TPU v7x, 128 devices: a whole 4x4x4 slice. The times are simulated.
128 devices in a mesh: row: 8 (over z_lo, y), col: 16 (over x, z_hi, core).
Axes of the slice: x: 4, y: 4, z: 4 (z_hi: 2, z_lo: 2; z = z_hi * 2 + z_lo), core: 2. Of those that a mesh axis runs over, the one named last changes fastest.
Arguments:
- view_a: bfloat16 [12288, 8192], P(('row', 'col')), may hold values from -1000 to 1000
- view_b: bfloat16 [12288, 8192], P(('row', 'col')), may hold values from -1000 to 1000
Outputs:
- correlation: float32 [8192, 8192], P('row', 'col')
- loss: float32 [], replicated
All inputs are finite; a program needn't handle non-finite values.
Results may differ from a plain program's by a relative error of at most 0.0013.
Values may be sent and summed in bfloat16 or wider, within the bound.
A program may use at most 192 MiB of HBM per device.

v0:
```python
import jax
import jax.numpy as jnp
from jax import lax
from jax.sharding import Mesh
from jax.sharding import PartitionSpec as P

ROW = ("row_0", "row_1")
COL = ("col_0", "col_1", "col_2")
ROW_COL = ("row_0", "row_1", "col_0", "col_1", "col_2")


def from_everyone(array, axis):
    length = lax.axis_size(axis)
    return lax.all_to_all(
        jnp.broadcast_to(array[None], (length, *array.shape)), axis, 0, 0, tiled=True
    )


def over_copies(array, axis):
    return from_everyone(array, axis).sum(axis=0)


def together(arrays, axis):
    vector, at, outs = (jnp.concatenate([a.reshape(-1) for a in arrays]), 0, [])
    subtotal = over_copies(vector, axis)
    for a in arrays:
        outs.append(subtotal[at : at + a.size].reshape(a.shape))
        at += a.size
    return tuple(outs)


def over_axes(array, axes):
    for axis in axes:
        array = lax.psum(array, axis)
    return array


def moments(view):
    values = view.astype(jnp.float32)
    return (jnp.sum(values, 0), jnp.sum(values * values, 0))


def scaled(view, total, squares, count):
    mean = total / count
    var = squares / count - mean * mean
    return ((view.astype(jnp.float32) - mean) * lax.rsqrt(var + 1e-05)).astype(jnp.bfloat16)


def shards(view_a, view_b):
    rows_local = view_a.shape[0]
    width = view_a.shape[1]
    n_row = lax.axis_size(ROW)
    n_col = lax.axis_size(COL)
    count = rows_local * n_row * n_col
    left = lax.all_to_all(view_a, ROW, split_axis=1, concat_axis=0, tiled=True)
    right = lax.all_to_all(view_b, COL, split_axis=1, concat_axis=0, tiled=True)
    part_total, part_squares = moments(left)
    part_total, part_squares = together((part_total, part_squares), COL)
    left = scaled(left, part_total, part_squares, count)
    side_total, side_squares = moments(right)
    side_total, side_squares = together((side_total, side_squares), ROW)
    right = scaled(right, side_total, side_squares, count)
    row_block = left.shape[1]
    col_block = right.shape[1]
    every_left = lax.all_gather(left, COL, axis=0, tiled=True)
    grouped = every_left.reshape(n_col, n_row, rows_local, row_block)
    piece = lax.all_gather(right, ROW, axis=0, tiled=True)
    groups = piece.shape[0] // right.shape[0]
    blocks = piece.reshape(groups, n_col, rows_local, col_block)
    product = jnp.einsum("ckbf,kcbg->fg", grouped, blocks, preferred_element_type=jnp.float32)
    correlation = product / count
    row_ids = lax.axis_index(ROW) * row_block + lax.broadcasted_iota(jnp.int32, (row_block, 1), 0)
    col_ids = lax.axis_index(COL) * col_block + lax.broadcasted_iota(jnp.int32, (1, col_block), 1)
    on_diag = row_ids == col_ids
    squared = correlation * correlation
    diag_terms = jnp.where(on_diag, (1.0 - correlation) ** 2 - 0.0051 * squared, 0.0)
    partial_loss = 0.0051 * jnp.sum(squared) + jnp.sum(diag_terms)
    loss = over_axes(partial_loss, ROW_COL) / width
    return (correlation, loss)


def solution(mesh):
    finer = Mesh(mesh.devices.reshape(2, 4, 4, 2, 2), ("row_0", "row_1", "col_0", "col_1", "col_2"))
    in_specs = (P(ROW_COL, None), P(ROW_COL, None))
    out_specs = (P(ROW, COL), P())
    return jax.shard_map(
        shards, mesh=finer, in_specs=in_specs, out_specs=out_specs, check_vma=False
    )
```

profile of v0, /device:TPU:1, one launch (start us, length us, event | category | flops | bytes accessed | tf_op | source)
XLA Modules:
  0.0 412.5 jit_solution(15244681674789364637)
XLA Ops:
  7.2 0.0 all-gather.5.cloned.1.call-start
  7.2 1.6 copy.40
  8.8 31.3 %all_to_all.38 = bf16[96,16,512]{2,0,1:T(8,128)(2,1)S(1)} all-to-all(bf16[96,16,512]{2,0,1:T(8,128)(2,1)S(1)} %bitcast.31), channel_id=1, replica_groups=mesh['row_0'=2,'row_1'=4,'col_0'=4,'col_1'=2,'col_2'=2] {'col_0','col_1'..., dimensions={1} | all-to-all | bytes 3145728 | tf_op jit(solution)/shard_map/all_to_all | solution.py:56
  40.1 0.5 convert_reduce_fusion
  40.6 9.6 %all_to_all.39 = f32[8,1,1024]{2,1,0:T(1,128)S(1)} all-to-all(f32[8,1,1024]{2,1,0:T(1,128)S(1)} %broadcast_in_dim.8), channel_id=1, replica_groups=mesh['row_0'=2,'row_1'=4,'col_0'=4,'col_1'=2,'col_2'=2] {'row_0','row_1'}, dimensions={0} | all-to-all | bytes 65536 | tf_op jit(solution)/shard_map/all_to_all | solution.py:14
  50.2 1.5 fusion.3
  51.8 0.0 all-gather.5.cloned.1.call-update
  51.8 0.0 all-gather.3.cloned.1.call-start
  51.9 0.1 copy.41
  52.0 29.4 %all_to_all.40 = bf16[96,8,1024]{2,0,1:T(8,128)(2,1)S(1)} all-to-all(bf16[96,8,1024]{2,0,1:T(8,128)(2,1)S(1)} %bitcast.32), channel_id=1, replica_groups=mesh['row_0'=2,'row_1'=4,'col_0'=4,'col_1'=2,'col_2'=2] {'row_0','row_1'}, dimensions={1} | all-to-all | bytes 3145728 | tf_op jit(solution)/shard_map/all_to_all | solution.py:55
  81.4 0.5 convert_reduce_fusion.1
  81.8 0.1 broadcast_in_dim.7
  81.9 114.3 %all_to_all.41 = f32[16,1,2048]{2,1,0:T(1,128)S(1)} all-to-all(f32[16,1,2048]{2,1,0:T(1,128)S(1)} %broadcast_in_dim.7), channel_id=1, replica_groups=mesh['row_0'=2,'row_1'=4,'col_0'=4,'col_1'=2,'col_2'=2] {'col_0','col_1'..., dimensions={0} | all-to-all | bytes 262144 | tf_op jit(solution)/shard_map/all_to_all | solution.py:14
  196.2 0.1 reduce_sum.74
  196.3 1.6 fusion.5
  197.9 0.0 all-gather.3.cloned.1.call-update
  198.0 0.0 all-gather.5.cloned.1.call-done
  198.0 145.5 %all-gather.3.cloned.1.call-done = bf16[12288,1024]{1,0:T(8,128)(2,1)} async-done(((bf16[768,1024]{1,0:T(8,128)(2,1)}), bf16[12288,1024]{1,0:T(8,128)(2,1)}) %all-gather.3.cloned.1.call-update) | async-done | bytes 25165840 | tf_op jit(solution)/shard_map/all_gather | solution.py:65
  343.5 23.4 %select_reduce_fusion = (f32[]{:T(128)}, f32[]{:T(128)}, f32[1024,512]{1,0:T(8,128)}) fusion(s32[512]{0:T(512)S(1)} %iota_add_fusion.1, s32[1024]{0:T(1024)S(1)} %iota_add_fusion, bf16[16,8,96,1024]{3,2,1,0:T(8,128)(2,1)} %bitcast.35, bf16[8,16,96,512]{3,2,1,0:T(8,128)(2,1)} %bitcast.36), kind=kOutput, calls=%fused_computation.11 | convolution fusion | flops 12890144768 | bytes 39852040 | tf_op jit(solution)/shard_map/ckbf,kcbg->fg/dot_general | solution.py:70
  368.2 4.3 %psum.35 = f32[]{:T(128)} all-reduce(f32[]{:T(128)S(6)} %add.67), channel_id=1, replica_groups=mesh['row_0'=2,'row_1'=4,'col_0'=4,'col_1'=2,'col_2'=2] {'row_0'}, use_global_device_ids=true, to_apply=%region_8.9 | all-reduce | flops 1 | bytes 8 | tf_op jit(solution)/shard_map/psum | solution.py:34
  372.5 9.1 %psum.36 = f32[]{:T(128)} all-reduce(f32[]{:T(128)} %psum.35), channel_id=1, replica_groups=mesh['row_0'=2,'row_1'=4,'col_0'=4,'col_1'=2,'col_2'=2] {'row_1'}, use_global_device_ids=true, to_apply=%region_9.10 | all-reduce | flops 1 | bytes 8 | tf_op jit(solution)/shard_map/psum | solution.py:34
  381.5 7.2 %psum.37 = f32[]{:T(128)} all-reduce(f32[]{:T(128)} %psum.36), channel_id=1, replica_groups=mesh['row_0'=2,'row_1'=4,'col_0'=4,'col_1'=2,'col_2'=2] {'col_0'}, use_global_device_ids=true, to_apply=%region_10.11 | all-reduce | flops 1 | bytes 8 | tf_op jit(solution)/shard_map/psum | solution.py:34
  388.7 5.9 %psum.38 = f32[]{:T(128)} all-reduce(f32[]{:T(128)} %psum.37), channel_id=1, replica_groups=mesh['row_0'=2,'row_1'=4,'col_0'=4,'col_1'=2,'col_2'=2] {'col_1'}, use_global_device_ids=true, to_apply=%region_11.12 | all-reduce | flops 1 | bytes 8 | tf_op jit(solution)/shard_map/psum | solution.py:34
  394.6 9.3 %psum.39 = f32[]{:T(128)} all-reduce(f32[]{:T(128)} %psum.38), channel_id=1, replica_groups=mesh['row_0'=2,'row_1'=4,'col_0'=4,'col_1'=2,'col_2'=2] {'col_2'}, use_global_device_ids=true, to_apply=%region_12.13 | all-reduce | flops 1 | bytes 8 | tf_op jit(solution)/shard_map/psum | solution.py:34
  (10 shorter events, 0.1 us)
Async XLA Ops:
  7.2 190.8 %all-gather.5.cloned.1.call-start = ((), (), s32[]{:S(2)}) async-start(), calls=%async_computation.5 | async-start | bytes 14155776 | tf_op jit(solution)/shard_map/all_gather | solution.py:67
  50.2 1.6 copy-start
  51.8 291.7 %all-gather.3.cloned.1.call-start = ((), (), s32[]{:S(2)}) async-start(), calls=%async_computation.4 | async-start | bytes 26738688 | tf_op jit(solution)/shard_map/all_gather | solution.py:65
Sparse Core Ops, SparseCore 0:
  51.9 143.8 all-gather.4
  198.8 144.6 all-gather.2
where the time goes:
time: 413 us
  blocking collectives  220 us (53%)
  waiting for transfers between devices  146 us (35%)
  matrix products  23.4 us (6%)
  between operations  17.2 us (4%)
  other arithmetic  4.21 us (1%)
    all_gather x1, waiting for transfers between devices, shards(): every_left = lax.all_gather(left, COL, axis=0, tiled=True)  145 us
    all_to_all x2, blocking collectives, from_everyone(): lax.all_to_all(jnp.broadcast_to(array[None], (length, *array.shape)), axi...  124 us
    psum x5, blocking collectives, over_axes(): array = lax.psum(array, axis)  35.7 us
    all_to_all x1, blocking collectives, shards(): right = lax.all_to_all(view_b, COL, split_axis=1, concat_axis=0, tiled=True)  31.3 us
    all_to_all x1, blocking collectives, shards(): left = lax.all_to_all(view_a, ROW, split_axis=1, concat_axis=0, tiled=True)  29.4 us
    dot_general x1, matrix products, shards(): jnp.einsum('ckbf,kcbg->fg', grouped, blocks, preferred_element_type=jnp.f...  23.4 us
  transfers between devices with their start and end apart: 2, of which 1 were waited for; matrix products, arithmetic and copies ran while one was open for 1% of the time, Pallas kernels for 0%

commit v1 on v0

v1 whole, which is shorter than its diff:
```python
import jax
import jax.numpy as jnp
from jax import lax
from jax.experimental import pallas as pl
from jax.experimental.pallas import tpu as pltpu
from jax.sharding import Mesh
from jax.sharding import PartitionSpec as P

ROW = ("row_0", "row_1")
COL = ("col_0", "col_1", "col_2")
ROW_COL = ("row_0", "row_1", "col_0", "col_1", "col_2")

MESH = pl.DeviceIdType.MESH
F32 = jnp.float32
BF16 = jnp.bfloat16
SENT = BF16

Q = 4
S = 96
AQ = 512
AH = 256
BQ = 256
BH = 128
G = 8
GS = 384
CELLS = Q * Q


def kernel(count, width, a_ref, b_ref, out_ref, loss_ref,
           av, bv, at, bn, psend, pown, precv, prelay,
           ma_mine, ma_in, ma_sum, ma_zin, mb_mine, mb_in, mb_sum, mb_zin, sta, stb,
           lo_mine, lo_in,
           s1a_s, s1a_r, s1b_s, s1b_r,
           aga_s, aga_r, rla_s, rla_r, dd_s, dd_r,
           agb_s, agb_r, rlb_s, rlb_r,
           nr_s, nr_r, fr_s, fr_r, ry_s, ry_r,
           mo_s, mo_r, lo_s, lo_r):
    zl, y, x, zh, c = (lax.axis_index(n) for n in ROW_COL)
    z = zh * 2 + zl

    def dev(x_=None, y_=None, z_=None, c_=None):
        zz = z if z_ is None else z_
        return (lax.rem(zz, 2), y if y_ is None else y_, x if x_ is None else x_,
                lax.div(zz, 2), c if c_ is None else c_)

    def ring(v, d):
        return lax.rem(v + d, 4)

    def xc(r):
        t = lax.rem(x * 2 + c + r, 8)
        return lax.div(t, 2), lax.rem(t, 2)

    def send(src, dst, ss, rs, device):
        cp = pltpu.make_async_remote_copy(src_ref=src, dst_ref=dst, send_sem=ss, recv_sem=rs,
                                          device_id=device, device_id_type=MESH)
        cp.start()

    def wait(ref, sem):
        pltpu.make_async_copy(ref, ref, sem).wait()

    x1, x2, x3 = ring(x, 1), ring(x, 2), ring(x, 3)
    y1, y2, y3 = ring(y, 1), ring(y, 2), ring(y, 3)
    z1, z2, z3 = ring(z, 1), ring(z, 2), ring(z, 3)
    other = 1 - c

    barrier = pltpu.get_barrier_semaphore()
    peers = [dev(y_=v) for v in (y1, y2, y3)] + [dev(z_=v) for v in (z1, z2, z3)]
    for r in range(1, 8):
        px, pc = xc(r)
        peers.append(dev(x_=px, c_=pc))
    for p in peers:
        pl.semaphore_signal(barrier, inc=1, device_id=p, device_id_type=MESH)
    pl.semaphore_wait(barrier, len(peers))

    def stage1(q, carry):
        for d in (1, 3, 2, 0):
            yp = ring(y, d)
            for h in range(2):
                src = a_ref.at[:, pl.ds(pl.multiple_of(h * 4096 + yp * 1024 + q * AH, AH), AH)]
                dst = av.at[q, x, y, c, :, pl.ds(h * AH, AH)]
                if d:
                    send(src, dst, s1a_s, s1a_r.at[q], dev(y_=yp))
                else:
                    pltpu.make_async_copy(src, dst, s1a_r.at[q]).start()
        for r in (1, 2, 3, 7, 6, 5, 4, 0):
            px, pc = xc(r)
            for h in range(2):
                src = b_ref.at[:, pl.ds(pl.multiple_of(px * 2048 + h * 1024 + pc * 512 + q * BH, BH), BH)]
                dst = bv.at[q, x, y, c, :, pl.ds(h * BH, BH)]
                if r:
                    send(src, dst, s1b_s, s1b_r.at[q], dev(x_=px, c_=pc))
                else:
                    pltpu.make_async_copy(src, dst, s1b_r.at[q]).start()
        return carry

    lax.fori_loop(0, Q, stage1, 0)

    def own(q):
        a = av.at[q, x, :, c]
        send(a, a, aga_s.at[q, 0], aga_r.at[q, 0], dev(x_=x1))
        send(a, a, aga_s.at[q, 1], aga_r.at[q, 1], dev(x_=x3))
        b = bv.at[q, :, y]
        send(b, b, agb_s.at[q, 0], agb_r.at[q, 0], dev(y_=y1))
        send(b, b, agb_s.at[q, 1], agb_r.at[q, 1], dev(y_=y3))
        send(a, a, dd_s.at[q, 0], dd_r.at[q, 0], dev(c_=other))

    def own_moments(q, carry):
        def one(k, acc):
            sa, qa, sb, qb = acc
            va = av[q, x, lax.div(k, 2), c, pl.ds(pl.multiple_of(lax.rem(k, 2) * 48, 16), 48), :].astype(F32)
            va = va.reshape(6, 8, AQ)
            sa = sa + jnp.sum(va, 0)
            qa = qa + jnp.sum(va * va, 0)
            vb = bv[q, lax.div(k, 2), y, lax.rem(k, 2)].astype(F32).reshape(12, 8, BQ)
            sb = sb + jnp.sum(vb, 0)
            qb = qb + jnp.sum(vb * vb, 0)
            return sa, qa, sb, qb

        za, zb = jnp.zeros((8, AQ), F32), jnp.zeros((8, BQ), F32)
        sa, qa, sb, qb = lax.fori_loop(0, 8, one, (za, za, zb, zb))
        ma_mine[q, 0:1, :] = jnp.sum(sa, 0, keepdims=True)
        ma_mine[q, 1:2, :] = jnp.sum(qa, 0, keepdims=True)
        mb_mine[q, 0:1, :] = jnp.sum(sb, 0, keepdims=True)
        mb_mine[q, 1:2, :] = jnp.sum(qb, 0, keepdims=True)
        return carry

    def s1_wait(q):
        wait(av.at[q, x, :, c], s1a_r.at[q])
        wait(bv.at[q, :, y], s1b_r.at[q])

    s1_wait(0)
    own(0)
    for q in range(1, Q):
        s1_wait(q)
    lax.fori_loop(0, Q, own_moments, 0)
    for r in range(1, 8):
        px, pc = xc(r)
        send(ma_mine, ma_in.at[r - 1], mo_s.at[0], mo_r.at[0], dev(x_=px, c_=pc))
    for r, v in ((1, y1), (2, y2), (3, y3)):
        send(mb_mine, mb_in.at[r - 1], mo_s.at[1], mo_r.at[1], dev(y_=v))
    own(1)
    wait(ma_in, mo_r.at[0])
    wait(mb_in, mo_r.at[1])
    ma_sum[...] = ma_mine[...] + jnp.sum(ma_in[...], 0)
    mb_sum[...] = mb_mine[...] + jnp.sum(mb_in[...], 0)
    for r, v in ((1, z1), (2, z2), (3, z3)):
        send(ma_sum, ma_zin.at[r - 1], mo_s.at[2], mo_r.at[2], dev(z_=v))
        send(mb_sum, mb_zin.at[r - 1], mo_s.at[3], mo_r.at[3], dev(z_=v))
    wait(ma_zin, mo_r.at[2])
    wait(mb_zin, mo_r.at[3])
    for mine, zin, st in ((ma_sum, ma_zin, sta), (mb_sum, mb_zin, stb)):
        for q in range(Q):
            total = mine[q] + zin[0, q] + zin[1, q] + zin[2, q]
            mean = total[0:1, :] / count
            var = total[1:2, :] / count - mean * mean
            st[q, 0:1, :] = mean
            st[q, 1:2, :] = lax.rsqrt(var + 1e-05)

    def arrive(q):
        wait(av.at[q, x3, :, c], aga_r.at[q, 0])
        a = av.at[q, x3, 0:2, c]
        send(a, a, rla_s.at[q, 0], rla_r.at[q, 0], dev(x_=x1))
        wait(av.at[q, x1, :, c], aga_r.at[q, 1])
        a = av.at[q, x1, 2:4, c]
        send(a, a, rla_s.at[q, 1], rla_r.at[q, 1], dev(x_=x3))
        wait(bv.at[q, :, y3], agb_r.at[q, 0])
        b = bv.at[q, 0:2, y3]
        send(b, b, rlb_s.at[q, 0], rlb_r.at[q, 0], dev(y_=y1))
        wait(bv.at[q, :, y1], agb_r.at[q, 1])
        b = bv.at[q, 2:4, y1]
        send(b, b, rlb_s.at[q, 1], rlb_r.at[q, 1], dev(y_=y3))
        for k, v in ((1, x3), (2, x1)):
            a = av.at[q, v, :, c]
            send(a, a, dd_s.at[q, k], dd_r.at[q, k], dev(c_=other))

    def far(q):
        wait(av.at[q, x2, 0:2, c], rla_r.at[q, 0])
        wait(av.at[q, x2, 2:4, c], rla_r.at[q, 1])
        a = av.at[q, x2, :, c]
        send(a, a, dd_s.at[q, 3], dd_r.at[q, 3], dev(c_=other))
        wait(bv.at[q, 0:2, y2], rlb_r.at[q, 0])
        wait(bv.at[q, 2:4, y2], rlb_r.at[q, 1])
        for k, v in ((0, x), (1, x3), (2, x1), (3, x2)):
            wait(av.at[q, v, :, other], dd_r.at[q, k])

    def normalise(q):
        def group(g, carry):
            x0, yh = lax.div(g, 2), lax.rem(g, 2)
            at_ = pl.multiple_of(g * GS, 128)
            for n in range(AQ // 128):
                cols = pl.ds(n * 128, 128)
                v = av[q, x0, pl.ds(yh * 2, 2), :, :, cols].reshape(GS, 128).astype(F32)
                v = ((v - sta[q, 0:1, cols]) * sta[q, 1:2, cols]).astype(BF16)
                at[q, cols, pl.ds(at_, GS)] = v.T
            for n in range(BQ // 128):
                cols = pl.ds(n * 128, 128)
                v = bv[q, x0, pl.ds(yh * 2, 2), :, :, cols].reshape(GS, 128).astype(F32)
                v = ((v - stb[q, 0:1, cols]) * stb[q, 1:2, cols]).astype(BF16)
                bn[q, pl.ds(at_, GS), cols] = v
            return carry

        lax.fori_loop(0, G, group, 0)

    def multiply(q):
        def cell(t, carry):
            i = jnp.where(t <= q, q, t - q - 1)
            j = jnp.where(t <= q, t, q)
            r = jnp.dot(at[i], bn[j], preferred_element_type=F32) * (1.0 / count)
            for h in range(2):
                for l in range(2):
                    block = r[l * AH:(l + 1) * AH, h * BH:(h + 1) * BH]
                    psend[h * 2 + l, q * q + t] = block.astype(SENT)

                    @pl.when(z == h * 2 + l)
                    def _():
                        pown[q * q + t] = block
            return carry

        lax.fori_loop(0, 2 * q + 1, cell, 0)

    def scatter(q):
        cells = pl.ds(q * q, 2 * q + 1)
        send(psend.at[z2, cells, 0:128], prelay.at[0, cells], fr_s.at[q, 0], fr_r.at[q, 0], dev(z_=z1))
        send(psend.at[z2, cells, 128:256], prelay.at[1, cells], fr_s.at[q, 1], fr_r.at[q, 1], dev(z_=z3))
        send(psend.at[z1, cells], precv.at[0, cells], nr_s.at[q, 0], nr_r.at[q, 0], dev(z_=z1))
        send(psend.at[z3, cells], precv.at[1, cells], nr_s.at[q, 1], nr_r.at[q, 1], dev(z_=z3))

    def pass_on(q):
        cells = pl.ds(q * q, 2 * q + 1)
        wait(prelay.at[0, cells], fr_r.at[q, 0])
        send(prelay.at[0, cells], precv.at[2, cells, 0:128], ry_s.at[q, 0], ry_r.at[q, 0], dev(z_=z1))
        wait(prelay.at[1, cells], fr_r.at[q, 1])
        send(prelay.at[1, cells], precv.at[2, cells, 128:256], ry_s.at[q, 1], ry_r.at[q, 1], dev(z_=z3))

    row0 = (zl * 4 + y) * 1024
    col0 = ((x * 2 + zh) * 2 + c) * 512

    def finish(q):
        cells = pl.ds(q * q, 2 * q + 1)
        wait(precv.at[0, cells], nr_r.at[q, 0])
        wait(precv.at[1, cells], nr_r.at[q, 1])
        wait(precv.at[2, cells, 0:128], ry_r.at[q, 0])
        wait(precv.at[2, cells, 128:256], ry_r.at[q, 1])

        def cell(t, carry):
            i = jnp.where(t <= q, q, t - q - 1)
            j = jnp.where(t <= q, t, q)
            k = q * q + t
            v = (pown[k] + precv[0, k].astype(F32)) + (precv[1, k].astype(F32) + precv[2, k].astype(F32))
            out_ref[pl.ds(pl.multiple_of(i * AH, AH), AH), pl.ds(pl.multiple_of(j * BH, BH), BH)] = v
            rows = row0 + i * AH + lax.broadcasted_iota(jnp.int32, (AH, BH), 0)
            cols = col0 + j * BH + lax.broadcasted_iota(jnp.int32, (AH, BH), 1)
            sq = v * v
            term = jnp.where(rows == cols, (1.0 - v) * (1.0 - v), 0.0051 * sq)
            lo_mine[0] += jnp.sum(term.reshape(AH // 8, 8, BH), 0)
            return carry

        lax.fori_loop(0, 2 * q + 1, cell, 0)

    lo_mine[...] = jnp.zeros_like(lo_mine)
    for q in range(Q):
        arrive(q)
        if q + 2 < Q:
            own(q + 2)
        if q:
            far(q - 1)
            normalise(q - 1)
            multiply(q - 1)
            scatter(q - 1)
            if q > 1:
                pass_on(q - 2)
    far(Q - 1)
    normalise(Q - 1)
    multiply(Q - 1)
    scatter(Q - 1)
    pass_on(Q - 2)
    for q in range(Q - 1):
        finish(q)
    pass_on(Q - 1)
    finish(Q - 1)

    base = 0
    for n, group in enumerate((
        [dev(x_=xc(r)[0], c_=xc(r)[1]) for r in range(1, 8)],
        [dev(y_=v) for v in (y1, y2, y3)],
        [dev(z_=v) for v in (z1, z2, z3)],
    )):
        for k, p in enumerate(group):
            send(lo_mine.at[n], lo_in.at[base + k], lo_s.at[n], lo_r.at[n], p)
        wait(lo_in.at[pl.ds(base, len(group))], lo_r.at[n])
        total = lo_mine[n]
        for k in range(len(group)):
            total = total + lo_in[base + k]
        if n < 2:
            lo_mine[n + 1] = total
        base += len(group)
    loss_ref[0, 0] = jnp.sum(total) / width

    wait(a_ref.at[:, 0:6144], s1a_s)
    wait(b_ref.at[:, 0:7168], s1b_s)
    for q in range(Q):
        for k in range(2):
            wait(av.at[q, x, :, c], aga_s.at[q, k])
            wait(bv.at[q, :, y], agb_s.at[q, k])
            wait(av.at[q, x, 0:2, c], rla_s.at[q, k])
            wait(bv.at[q, 0:2, y], rlb_s.at[q, k])
            cells = pl.ds(q * q, 2 * q + 1)
            wait(precv.at[0, cells], nr_s.at[q, k])
            wait(prelay.at[0, cells], fr_s.at[q, k])
            wait(prelay.at[0, cells], ry_s.at[q, k])
        for k in range(4):
            wait(av.at[q, x, :, c], dd_s.at[q, k])
    wait(ma_in, mo_s.at[0])
    wait(mb_in, mo_s.at[1])
    wait(ma_zin, mo_s.at[2])
    wait(mb_zin, mo_s.at[3])
    wait(lo_in.at[0:7], lo_s.at[0])
    wait(lo_in.at[0:3], lo_s.at[1])
    wait(lo_in.at[0:3], lo_s.at[2])


def shards(view_a, view_b):
    rows, width = view_a.shape
    count = rows * 128
    dma = pltpu.SemaphoreType.DMA
    vm = pltpu.VMEM
    out, loss = pl.pallas_call(
        lambda *refs: kernel(float(count), float(width), *refs),
        out_shape=(jax.ShapeDtypeStruct((1024, 512), F32), jax.ShapeDtypeStruct((1, 1), F32)),
        in_specs=[pl.BlockSpec(memory_space=pl.ANY)] * 2,
        out_specs=(pl.BlockSpec(memory_space=pltpu.VMEM), pl.BlockSpec(memory_space=pltpu.SMEM)),
        scratch_shapes=[
            vm((Q, 4, 4, 2, S, AQ), BF16),
            vm((Q, 4, 4, 2, S, BQ), BF16),
            vm((Q, AQ, G * GS), BF16),
            vm((Q, G * GS, BQ), BF16),
            vm((4, CELLS, AH, BH), SENT),
            vm((CELLS, AH, BH), F32),
            vm((3, CELLS, AH, BH), SENT),
            vm((2, CELLS, AH // 2, BH), SENT),
            vm((Q, 2, AQ), F32), vm((7, Q, 2, AQ), F32), vm((Q, 2, AQ), F32), vm((3, Q, 2, AQ), F32),
            vm((Q, 2, BQ), F32), vm((3, Q, 2, BQ), F32), vm((Q, 2, BQ), F32), vm((3, Q, 2, BQ), F32),
            vm((Q, 2, AQ), F32), vm((Q, 2, BQ), F32),
            vm((3, 8, 128), F32), vm((13, 8, 128), F32),
            dma, dma((Q,)), dma, dma((Q,)),
            dma((Q, 2)), dma((Q, 2)), dma((Q, 2)), dma((Q, 2)), dma((Q, 4)), dma((Q, 4)),
            dma((Q, 2)), dma((Q, 2)), dma((Q, 2)), dma((Q, 2)),
            dma((Q, 2)), dma((Q, 2)), dma((Q, 2)), dma((Q, 2)), dma((Q, 2)), dma((Q, 2)),
            dma((4,)), dma((4,)), dma((3,)), dma((3,)),
        ],
        compiler_params=pltpu.CompilerParams(
            collective_id=0, has_side_effects=True, vmem_limit_bytes=67_000_000),
    )(view_a, view_b)
    return out, loss.reshape(())


def solution(mesh):
    finer = Mesh(mesh.devices.reshape(2, 4, 4, 2, 2), ROW_COL)
    in_specs = (P(ROW_COL, None), P(ROW_COL, None))
    out_specs = (P(ROW, COL), P())
    return jax.shard_map(
        shards, mesh=finer, in_specs=in_specs, out_specs=out_specs, check_vma=False
    )
```

time: 413 us -> 143 us (0.35)
  blocking collectives: 220 us -> 0 us
  waiting for transfers between devices: 146 us -> 0 us
  Pallas kernels: 0 us -> 137 us
  matrix products: 23.4 us -> 0 us
  between operations: 17.2 us -> 2.37 us
  other arithmetic: 4.21 us -> 0 us
    all_to_all x4 -> x0, blocking collectives: 185 us -> none  [the longest x2 124 us: from_everyone(): lax.all_to_all(jnp.broadcast_to(array[None], (length, *array.shape)), axi...]
    all_gather x2 -> x0, waiting for transfers between devices: 145 us -> none  [the longest x1 145 us: shards(): every_left = lax.all_gather(left, COL, axis=0, tiled=True)]
    pallas_call x0 -> x1, Pallas kernels: none -> 137 us  [shards(): pl.pallas_call(lambda *refs: kernel(float(count), float(width), *refs), o...]
    psum x5 -> x0, blocking collectives: 35.7 us -> none  [over_axes(): array = lax.psum(array, axis)]
    dot_general x1 -> x0, matrix products: 23.4 us -> none  [shards(): jnp.einsum('ckbf,kcbg->fg', grouped, blocks, preferred_element_type=jnp.f...]
  transfers between devices with their start and end apart: 2 -> 0, of which waited for: 1 -> 0; matrix products, arithmetic and copies ran while one was open for 1% -> 0% of each run, Pallas kernels for 0% -> 0%
where the time goes in v1:
time: 143 us
  Pallas kernels  137 us (96%)
  local copies, waits for them, and re-layouts  3.08 us (2%)
  between operations  2.37 us (2%)
    pallas_call x1, Pallas kernels, shards(): pl.pallas_call(lambda *refs: kernel(float(count), float(width), *refs), o...  137 us
    unnamed x1, local copies, waits for them, and re-layouts  3.08 us

profile of v1, /device:TPU:1, one launch (start us, length us, event | category | flops | bytes accessed | tf_op | source)
XLA Modules:
  0.0 142.7 jit_solution(9795129087531575675)
XLA Ops:
  0.6 137.2 %shard_map.41 = (f32[1024,512]{1,0:T(8,128)}, f32[1,1]{1,0:T(1,128)}) custom-call(bf16[96,8192]{1,0:T(8,128)(2,1)} %refs_0_.1, bf16[96,8192]{1,0:T(8,128)(2,1)} %refs_1_.1), custom_call_target="tpu_custom_call" | custom-call | tf_op jit(solution)/shard_map/pallas_call | solution.py:327
  137.9 3.1 %copy.6 = f32[1024,512]{1,0:T(8,128)} copy(f32[1024,512]{1,0:T(8,128)} %get-tuple-element.8) | data formatting | bytes 4194304

commit v2 on v0

v2 whole, which is shorter than its diff:
```python
import jax
import jax.numpy as jnp
from jax import lax
from jax.experimental import pallas as pl
from jax.experimental.pallas import tpu as pltpu
from jax.sharding import Mesh
from jax.sharding import PartitionSpec as P

ROW = ("row_0", "row_1")
COL = ("col_0", "col_1", "col_2")
ROW_COL = ("row_0", "row_1", "col_0", "col_1", "col_2")

MESH = pl.DeviceIdType.MESH
F32 = jnp.float32
BF16 = jnp.bfloat16

N = 8
S = 96
AW = 256
BW = 128
GS = 384
K = 3072


def kernel(count, width, a_ref, b_ref, out_ref, loss_ref,
           av, bv, at, bn, psend, precv, prelay,
           ma_mine, ma_in, ma_sum, ma_zin, mb_mine, mb_in, mb_sum, mb_zin, sta, stb,
           lo_sum, lo_mine, lo_in,
           s1a_s, s1a_r, s1b_s, s1b_r,
           aga_s, aga_r, rla_s, rla_r, dd_s, dd_r,
           agb_s, agb_r, rlb_s, rlb_r,
           z1_s, z1_r, z3_s, z3_r, fr_s, fr_r, ry_s, ry_r,
           mo_s, mo_r, lo_s, lo_r):
    zl, y, x, zh, c = (lax.axis_index(n) for n in ROW_COL)

    def scoped(f):
        def g(q, *rest):
            with jax.named_scope(f"{f.__name__}_{q}"):
                return f(q, *rest)
        return g

    def dev(x_=None, y_=None, c_=None, zl_=None, zh_=None):
        return (zl if zl_ is None else zl_, y if y_ is None else y_, x if x_ is None else x_,
                zh if zh_ is None else zh_, c if c_ is None else c_)

    def ring(v, d):
        return lax.rem(v + d, 4)

    def xc(r):
        t = lax.rem(x * 2 + c + r, 8)
        return lax.div(t, 2), lax.rem(t, 2)

    def send(src, dst, ss, rs, device):
        pltpu.make_async_remote_copy(src_ref=src, dst_ref=dst, send_sem=ss, recv_sem=rs,
                                     device_id=device, device_id_type=MESH).start()

    def wait(ref, sem):
        pltpu.make_async_copy(ref, ref, sem).wait()

    x1, x2, x3 = ring(x, 1), ring(x, 2), ring(x, 3)
    y1, y2, y3 = ring(y, 1), ring(y, 2), ring(y, 3)
    other = 1 - c
    p1 = dev(zl_=1 - zl)
    p2 = dev(zh_=1 - zh)
    p3 = dev(zl_=1 - zl, zh_=1 - zh)
    xcs = [dev(x_=xc(r)[0], c_=xc(r)[1]) for r in range(1, 8)]
    ys = [dev(y_=v) for v in (y1, y2, y3)]
    zs = [p1, p2, p3]
    plane = []
    for r in range(1, 32):
        px, pc = xc(r % 8)
        plane.append(dev(x_=px, y_=ring(y, r // 8), c_=pc))

    barrier = pltpu.get_barrier_semaphore()
    peers = xcs + ys + zs
    with jax.named_scope("barrier"):
        for p in peers:
            pl.semaphore_signal(barrier, inc=1, device_id=p, device_id_type=MESH)
        pl.semaphore_wait(barrier, len(peers))

    def stage1(n, carry):
        k = lax.rem(n, 4)
        ha = lax.rem(zl + lax.div(n, 4), 2)
        hb = lax.rem(zh + 1 + lax.div(n, 4), 2)
        for d in (1, 3, 2, 0):
            yp = ring(y, d)
            src = a_ref.at[:, pl.ds(pl.multiple_of(ha * 4096 + yp * 1024 + k * AW, AW), AW)]
            dst = av.at[n, x, y, c]
            if d:
                send(src, dst, s1a_s, s1a_r.at[n], dev(y_=yp))
            else:
                pltpu.make_async_copy(src, dst, s1a_r.at[n]).start()
        for r in (1, 2, 3, 7, 6, 5, 4, 0):
            px, pc = xc(r)
            src = b_ref.at[:, pl.ds(pl.multiple_of(px * 2048 + hb * 1024 + pc * 512 + k * BW, BW), BW)]
            dst = bv.at[n, x, y, c]
            if r:
                send(src, dst, s1b_s, s1b_r.at[n], dev(x_=px, c_=pc))
            else:
                pltpu.make_async_copy(src, dst, s1b_r.at[n]).start()
        return carry

    with jax.named_scope("stage1"):
        lax.fori_loop(0, N, stage1, 0)

    def s1_wait(n):
        wait(av.at[n, x, :, c], s1a_r.at[n])
        wait(bv.at[n, :, y], s1b_r.at[n])

    @scoped
    def own(n, lo=0, hi=4):
        part = pl.ds(lo, hi - lo)
        a = av.at[n, x, part, c]
        send(a, a, aga_s.at[n, 0], aga_r.at[n, 0], dev(x_=x1))
        send(a, a, aga_s.at[n, 1], aga_r.at[n, 1], dev(x_=x3))
        b = bv.at[n, part, y]
        send(b, b, agb_s.at[n, 0], agb_r.at[n, 0], dev(y_=y1))
        send(b, b, agb_s.at[n, 1], agb_r.at[n, 1], dev(y_=y3))
        send(a, a, dd_s.at[n, 0], dd_r.at[n, 0], dev(c_=other))

    def own_moments(n):
        def one(k, acc):
            sa, qa, sb, qb = acc
            va = av[n, x, lax.div(k, 2), c, pl.ds(pl.multiple_of(lax.rem(k, 2) * 48, 16), 48), :].astype(F32)
            va = va.reshape(6, 8, AW)
            sa = sa + jnp.sum(va, 0)
            qa = qa + jnp.sum(va * va, 0)
            vb = bv[n, lax.div(k, 2), y, lax.rem(k, 2)].astype(F32).reshape(12, 8, BW)
            sb = sb + jnp.sum(vb, 0)
            qb = qb + jnp.sum(vb * vb, 0)
            return sa, qa, sb, qb

        za, zb = jnp.zeros((8, AW), F32), jnp.zeros((8, BW), F32)
        sa, qa, sb, qb = lax.fori_loop(0, 8, one, (za, za, zb, zb))
        ma_mine[n, 0:1, :] = jnp.sum(sa, 0, keepdims=True)
        ma_mine[n, 1:2, :] = jnp.sum(qa, 0, keepdims=True)
        mb_mine[n, 0:1, :] = jnp.sum(sb, 0, keepdims=True)
        mb_mine[n, 1:2, :] = jnp.sum(qb, 0, keepdims=True)

    @scoped
    def arrive(n):
        wait(av.at[n, x3, :, c], aga_r.at[n, 0])
        a = av.at[n, x3, 0:2, c]
        send(a, a, rla_s.at[n, 0], rla_r.at[n, 0], dev(x_=x1))
        wait(av.at[n, x1, :, c], aga_r.at[n, 1])
        a = av.at[n, x1, 2:4, c]
        send(a, a, rla_s.at[n, 1], rla_r.at[n, 1], dev(x_=x3))
        wait(bv.at[n, :, y3], agb_r.at[n, 0])
        b = bv.at[n, 0:2, y3]
        send(b, b, rlb_s.at[n, 0], rlb_r.at[n, 0], dev(y_=y1))
        wait(bv.at[n, :, y1], agb_r.at[n, 1])
        b = bv.at[n, 2:4, y1]
        send(b, b, rlb_s.at[n, 1], rlb_r.at[n, 1], dev(y_=y3))
        for k, v in ((1, x3), (2, x1)):
            a = av.at[n, v, :, c]
            send(a, a, dd_s.at[n, k], dd_r.at[n, k], dev(c_=other))

    def wait_and_sum(n, carry):
        s1_wait(n)
        own_moments(n)
        return carry

    with jax.named_scope("s1_wait"):
        s1_wait(0)
        own(0)
        own_moments(0)
        lax.fori_loop(1, N, wait_and_sum, 0)
    for r, p in enumerate(xcs):
        send(ma_mine, ma_in.at[r], mo_s.at[0], mo_r.at[0], p)
    for r, p in enumerate(ys):
        send(mb_mine, mb_in.at[r], mo_s.at[1], mo_r.at[1], p)
    own(1)
    arrive(0)
    own(2)
    with jax.named_scope("mom_1"):
        wait(ma_in, mo_r.at[0])
        wait(mb_in, mo_r.at[1])
    ma_sum[...] = ma_mine[...] + jnp.sum(ma_in[...], 0)
    mb_sum[...] = mb_mine[...] + jnp.sum(mb_in[...], 0)
    for r, p in enumerate(zs):
        send(ma_sum, ma_zin.at[r], mo_s.at[2], mo_r.at[2], p)
        send(mb_sum, mb_zin.at[r], mo_s.at[3], mo_r.at[3], p)
    arrive(1)
    own(3)

    def moments_done():
        with jax.named_scope("mom_2"):
            wait(ma_zin, mo_r.at[2])
            wait(mb_zin, mo_r.at[3])
        for mine, zin, st, turn in ((ma_sum, ma_zin, sta, (4, 0, 4)), (mb_sum, mb_zin, stb, (0, 4, 4))):
            for n in range(N):
                total = mine[n] + zin[0, (n + turn[0]) % N] + zin[1, (n + turn[1]) % N] + zin[2, (n + turn[2]) % N]
                mean = total[0:1, :] / count
                var = total[1:2, :] / count - mean * mean
                st[n, 0:1, :] = mean
                st[n, 1:2, :] = lax.rsqrt(var + 1e-05)

    @scoped
    def far(n):
        wait(av.at[n, x2, 0:2, c], rla_r.at[n, 0])
        wait(av.at[n, x2, 2:4, c], rla_r.at[n, 1])
        a = av.at[n, x2, :, c]
        send(a, a, dd_s.at[n, 3], dd_r.at[n, 3], dev(c_=other))
        wait(bv.at[n, 0:2, y2], rlb_r.at[n, 0])
        wait(bv.at[n, 2:4, y2], rlb_r.at[n, 1])

    def norm_a(n, lo, hi):
        def group(g, carry):
            x0, yh = ring(x2 + 1, lax.div(g, 2)), lax.rem(g, 2)
            at_ = pl.multiple_of((x0 * 2 + yh) * GS, 128)
            for m in range(AW // 128):
                cols = pl.ds(m * 128, 128)
                v = av[n, x0, pl.ds(yh * 2, 2), :, :, cols].reshape(GS, 128).astype(F32)
                v = ((v - sta[n, 0:1, cols]) * sta[n, 1:2, cols]).astype(BF16)
                at[n, cols, pl.ds(at_, GS)] = v.T
            return carry

        lax.fori_loop(lo, hi, group, 0)

    def norm_b(n, lo, hi):
        cols = pl.ds((n % 4) * BW, BW)

        def group(g, carry):
            x0, yh = lax.rem(g, 4), lax.rem(lax.div(y2, 2) + 1 + lax.div(g, 4), 2)
            at_ = pl.multiple_of((x0 * 2 + yh) * GS, 128)
            v = bv[n, x0, pl.ds(yh * 2, 2)].reshape(GS, BW).astype(F32)
            v = ((v - stb[n, 0:1, :]) * stb[n, 1:2, :]).astype(BF16)
            bn[n // 4, pl.ds(at_, GS), cols] = v
            return carry

        lax.fori_loop(lo, hi, group, 0)

    @scoped
    def near_norm(n):
        for k, v in ((0, x), (1, x3), (2, x1)):
            wait(av.at[n, v, :, other], dd_r.at[n, k])
        norm_a(n, 0, 6)
        norm_b(n, 0, 4)

    @scoped
    def far_norm(n):
        wait(av.at[n, x2, :, other], dd_r.at[n, 3])
        norm_a(n, 6, 8)
        norm_b(n, 4, 8)

    def dot(i, half, j, n):
        r = jnp.dot(at[i], bn[half, :, j * BW:(j + n) * BW], preferred_element_type=F32)
        return r * (1.0 / count)

    def row(slot, m, i, half, n):
        r = dot(i, half, 0, n)
        for j in range(n):
            psend[slot, m, j] = r[:, j * BW:(j + 1) * BW].astype(BF16)

    def column(slot, m, base, half):
        def one(i, carry):
            psend[slot, i, m] = dot(base + i, half, m, 1).astype(BF16)
            return carry

        lax.fori_loop(0, m, one, 0)

    def parts(m):
        yield 0, (m, pl.ds(0, m + 1))
        if m:
            yield 1, (pl.ds(0, m), m)

    HALVES = ((0, pl.ds(0, 128)), (1, pl.ds(128, 128)))

    @scoped
    def multiply_far(m):
        row(1, m, m, 0, m + 1)
        column(1, m, 0, 0)
        for k, cells in parts(m):
            for h, rows in HALVES:
                send(psend.at[(1, *cells, rows)], prelay.at[(h, *cells)],
                     fr_s.at[m, k, h], fr_r.at[m, k, h], (p1, p3)[h])

    def send_1(m, k):
        for kk, cells in parts(m):
            if kk == k:
                send(psend.at[(0, *cells)], precv.at[(0, *cells)], z1_s.at[m, k], z1_r.at[m, k], p1)

    @scoped
    def row_1(n):
        row(0, n - 4, n, 1, n - 3)
        send_1(n - 4, 0)

    @scoped
    def column_1(n):
        column(0, n - 4, 4, 1)
        send_1(n - 4, 1)

    @scoped
    def multiply_3(n):
        m = n % 4
        row(2, m, n, 0, 4)
        send(psend.at[2, m], precv.at[2, m], z3_s.at[m], z3_r.at[m], p3)

    @scoped
    def pass_on(m):
        for k, cells in parts(m):
            for h, rows in HALVES:
                src = prelay.at[(h, *cells)]
                wait(src, fr_r.at[m, k, h])
                send(src, precv.at[(1, *cells, rows)], ry_s.at[m, k, h], ry_r.at[m, k, h], (p3, p1)[h])

    row0 = (zl * 4 + y) * 1024
    col0 = ((x * 2 + zh) * 2 + c) * 512

    def finish(i, j):
        at_ = (pl.ds(pl.multiple_of(i * AW, AW), AW), pl.ds(pl.multiple_of(j * BW, BW), BW))
        v = out_ref[at_] + precv[1, i, j].astype(F32) + precv[2, i, j].astype(F32) + precv[0, i, j].astype(F32)
        out_ref[at_] = v
        rows = row0 + i * AW + lax.broadcasted_iota(jnp.int32, (AW, BW), 0)
        cols = col0 + j * BW + lax.broadcasted_iota(jnp.int32, (AW, BW), 1)
        term = jnp.where(rows == cols, (1.0 - v) * (1.0 - v), 0.0051 * (v * v))
        lo_sum[...] += jnp.sum(term.reshape(AW // 8, 8, BW), 0)

    lo_sum[...] = jnp.zeros_like(lo_sum)
    moments_done()
    for n in range(1, N - 1):
        if n > 1:
            arrive(n)
            if n + 2 < N - 1:
                own(n + 2)
            elif n + 2 == N - 1:
                own(N - 1, 0, 2)
            else:
                own(N - 1, 2, 4)
        near_norm(n - 1)
        far(n - 1)
        if n == 6:
            pass_on(3)
        far_norm(n - 1)
        if n < 5:
            multiply_far(n - 1)
        else:
            row_1(n - 1)
            column_1(n - 1)
            multiply_3(n - 1)
        if 2 <= n < 5:
            pass_on(n - 2)
    near_norm(N - 2)
    far(N - 2)
    arrive(N - 1)
    far_norm(N - 2)
    row_1(N - 2)
    far(N - 1)
    column_1(N - 2)
    near_norm(N - 1)
    far_norm(N - 1)
    multiply_3(N - 2)
    row_1(N - 1)
    column_1(N - 1)
    multiply_3(N - 1)

    with jax.named_scope("mine"):
        def mine(i, carry):
            out_ref[pl.ds(pl.multiple_of(i * AW, AW), AW), :] = dot(i, 1, 0, 4)
            return carry

        lax.fori_loop(0, 4, mine, 0)

    def z1_wait(m):
        for k, cells in parts(m):
            wait(precv.at[(0, *cells)], z1_r.at[m, k])

    with jax.named_scope("finish_early"):
        for m in range(4):
            for k, cells in parts(m):
                for h, rows in HALVES:
                    wait(precv.at[(1, *cells, rows)], ry_r.at[m, k, h])
        for m in range(3):
            wait(precv.at[2, m], z3_r.at[m])
            z1_wait(m)

        def early(t, carry):
            finish(lax.div(t, 3), lax.rem(t, 3))
            return carry

        lax.fori_loop(0, 9, early, 0)
    with jax.named_scope("finish_late"):
        wait(precv.at[2, 3], z3_r.at[3])
        z1_wait(3)

        def late(t, carry):
            finish(jnp.where(t < 4, 3, t - 4), jnp.where(t < 4, t, 3))
            return carry

        lax.fori_loop(0, 7, late, 0)

    lo_mine[0] = jnp.sum(lo_sum[...], 0, keepdims=True)
    base = 0
    for k, group in enumerate((plane, zs)):
        for r, p in enumerate(group):
            send(lo_mine.at[k], lo_in.at[base + r], lo_s.at[k], lo_r.at[k], p)
        with jax.named_scope(f"loss_{k}"):
            wait(lo_in.at[pl.ds(base, len(group))], lo_r.at[k])
        total = lo_mine[k] + jnp.sum(lo_in[pl.ds(base, len(group))], 0)
        if k == 0:
            lo_mine[1] = total
        base += len(group)
    loss_ref[0, 0] = jnp.sum(total) / width

    with jax.named_scope("drain"):
        wait(a_ref.at[:, 0:6144], s1a_s)
        wait(b_ref.at[:, 0:7168], s1b_s)
        for n in range(N):
            for k in range(2):
                wait(av.at[n, x, :, c], aga_s.at[n, k])
                wait(bv.at[n, :, y], agb_s.at[n, k])
                wait(av.at[n, x, 0:2, c], rla_s.at[n, k])
                wait(bv.at[n, 0:2, y], rlb_s.at[n, k])
            for k in range(4):
                wait(av.at[n, x, :, c], dd_s.at[n, k])
        for m in range(4):
            for k, cells in parts(m):
                wait(precv.at[(0, *cells)], z1_s.at[m, k])
                for h, rows in HALVES:
                    wait(prelay.at[(h, *cells)], fr_s.at[m, k, h])
                    wait(prelay.at[(h, *cells)], ry_s.at[m, k, h])
            wait(precv.at[2, m], z3_s.at[m])
        wait(ma_in, mo_s.at[0])
        wait(mb_in, mo_s.at[1])
        wait(ma_zin, mo_s.at[2])
        wait(mb_zin, mo_s.at[3])
        wait(lo_in.at[0:31], lo_s.at[0])
        wait(lo_in.at[0:3], lo_s.at[1])


def shards(view_a, view_b):
    rows, width = view_a.shape
    count = rows * 128
    dma = pltpu.SemaphoreType.DMA
    vm = pltpu.VMEM
    out, loss = pl.pallas_call(
        lambda *refs: kernel(float(count), float(width), *refs),
        out_shape=(pltpu.VMEM((1024, 512), F32), jax.ShapeDtypeStruct((1, 1), F32)),
        in_specs=[pl.BlockSpec(memory_space=pl.ANY)] * 2,
        out_specs=(pl.BlockSpec(memory_space=pltpu.VMEM), pl.BlockSpec(memory_space=pltpu.SMEM)),
        scratch_shapes=[
            vm((N, 4, 4, 2, S, AW), BF16),
            vm((N, 4, 4, 2, S, BW), BF16),
            vm((N, AW, K), BF16),
            vm((2, K, 4 * BW), BF16),
            vm((3, 4, 4, AW, BW), BF16),
            vm((3, 4, 4, AW, BW), BF16),
            vm((2, 4, 4, AW // 2, BW), BF16),
            vm((N, 2, AW), F32), vm((7, N, 2, AW), F32), vm((N, 2, AW), F32), vm((3, N, 2, AW), F32),
            vm((N, 2, BW), F32), vm((3, N, 2, BW), F32), vm((N, 2, BW), F32), vm((3, N, 2, BW), F32),
            vm((N, 2, AW), F32), vm((N, 2, BW), F32),
            vm((8, 128), F32), vm((2, 1, 128), F32), vm((34, 1, 128), F32),
            dma, dma((N,)), dma, dma((N,)),
            dma((N, 2)), dma((N, 2)), dma((N, 2)), dma((N, 2)), dma((N, 4)), dma((N, 4)),
            dma((N, 2)), dma((N, 2)), dma((N, 2)), dma((N, 2)),
            dma((4, 2)), dma((4, 2)), dma((4,)), dma((4,)),
            dma((4, 2, 2)), dma((4, 2, 2)), dma((4, 2, 2)), dma((4, 2, 2)),
            dma((4,)), dma((4,)), dma((2,)), dma((2,)),
        ],
        compiler_params=pltpu.CompilerParams(
            collective_id=0, has_side_effects=True, vmem_limit_bytes=56_000_000),
    )(view_a, view_b)
    return out, loss.reshape(())


def solution(mesh):
    finer = Mesh(mesh.devices.reshape(2, 4, 4, 2, 2), ROW_COL)
    in_specs = (P(ROW_COL, None), P(ROW_COL, None))
    out_specs = (P(ROW, COL), P())
    return jax.shard_map(
        shards, mesh=finer, in_specs=in_specs, out_specs=out_specs, check_vma=False
    )
```

time: 413 us -> 116 us (0.28)
  blocking collectives: 220 us -> 0 us
  waiting for transfers between devices: 146 us -> 0 us
  Pallas kernels: 0 us -> 112 us
  matrix products: 23.4 us -> 0 us
  between operations: 17.2 us -> 2.33 us
  other arithmetic: 4.21 us -> 0 us
    all_to_all x4 -> x0, blocking collectives: 185 us -> none  [the longest x2 124 us: from_everyone(): lax.all_to_all(jnp.broadcast_to(array[None], (length, *array.shape)), axi...]
    all_gather x2 -> x0, waiting for transfers between devices: 145 us -> none  [the longest x1 145 us: shards(): every_left = lax.all_gather(left, COL, axis=0, tiled=True)]
    pallas_call x0 -> x1, Pallas kernels: none -> 112 us  [shards(): pl.pallas_call(lambda *refs: kernel(float(count), float(width), *refs), o...]
    psum x5 -> x0, blocking collectives: 35.7 us -> none  [over_axes(): array = lax.psum(array, axis)]
    dot_general x1 -> x0, matrix products: 23.4 us -> none  [shards(): jnp.einsum('ckbf,kcbg->fg', grouped, blocks, preferred_element_type=jnp.f...]
  transfers between devices with their start and end apart: 2 -> 0, of which waited for: 1 -> 0; matrix products, arithmetic and copies ran while one was open for 1% -> 0% of each run, Pallas kernels for 0% -> 0%
where the time goes in v2:
time: 116 us; the launch traced here: 115 us
  Pallas kernels  112 us (97%)
  between operations  2.33 us (2%)
  local copies, waits for them, and re-layouts  1.32 us (1%)
    pallas_call x1, Pallas kernels, shards(): pl.pallas_call(lambda *refs: kernel(float(count), float(width), *refs), o...  112 us

profile of v2, /device:TPU:1, one launch (start us, length us, event | category | flops | bytes accessed | tf_op | source)
XLA Modules:
  0.0 115.3 jit_solution(6215448343618781466)
XLA Ops:
  0.6 111.7 %shard_map.41 = (f32[1024,512]{1,0:T(8,128)S(1)}, f32[1,1]{1,0:T(1,128)}) custom-call(bf16[96,8192]{1,0:T(8,128)(2,1)} %refs_0_.1, bf16[96,8192]{1,0:T(8,128)(2,1)} %refs_1_.1), custom_call_target="tpu_custom_call" | custom-call | tf_op jit(solution)/shard_map/pallas_call | solution.py:436
  112.3 1.3 %copy.6 = f32[1024,512]{1,0:T(8,128)} copy(f32[1024,512]{1,0:T(8,128)S(1)} %get-tuple-element.6) | data formatting | bytes 4194304

commit v3 on v2

--- a/solution.py
+++ b/solution.py
@@ -22,8 +22,8 @@
 K = 3072
 
 
-def kernel(count, width, a_ref, b_ref, out_ref, loss_ref,
-           av, bv, at, bn, psend, precv, prelay,
+def kernel(count, width, a_hbm, b_hbm, out_ref, loss_ref,
+           a_ref, b_ref, in_s, av, bv, at, bn, psend, precv, prelay,
            ma_mine, ma_in, ma_sum, ma_zin, mb_mine, mb_in, mb_sum, mb_zin, sta, stb,
            lo_sum, lo_mine, lo_in,
            s1a_s, s1a_r, s1b_s, s1b_r,
@@ -66,10 +66,10 @@
     xcs = [dev(x_=xc(r)[0], c_=xc(r)[1]) for r in range(1, 8)]
     ys = [dev(y_=v) for v in (y1, y2, y3)]
     zs = [p1, p2, p3]
-    plane = []
-    for r in range(1, 32):
-        px, pc = xc(r % 8)
-        plane.append(dev(x_=px, y_=ring(y, r // 8), c_=pc))
+    load_a = pltpu.make_async_copy(a_hbm, a_ref, in_s.at[0])
+    load_b = pltpu.make_async_copy(b_hbm, b_ref, in_s.at[1])
+    load_a.start()
+    load_b.start()
 
     barrier = pltpu.get_barrier_semaphore()
     peers = xcs + ys + zs
@@ -77,6 +77,8 @@
         for p in peers:
             pl.semaphore_signal(barrier, inc=1, device_id=p, device_id_type=MESH)
         pl.semaphore_wait(barrier, len(peers))
+    load_a.wait()
+    load_b.wait()
 
     def stage1(n, carry):
         k = lax.rem(n, 4)
@@ -84,20 +86,20 @@
         hb = lax.rem(zh + 1 + lax.div(n, 4), 2)
         for d in (1, 3, 2, 0):
             yp = ring(y, d)
-            src = a_ref.at[:, pl.ds(pl.multiple_of(ha * 4096 + yp * 1024 + k * AW, AW), AW)]
+            cols = pl.ds(pl.multiple_of(ha * 4096 + yp * 1024 + k * AW, AW), AW)
             dst = av.at[n, x, y, c]
             if d:
-                send(src, dst, s1a_s, s1a_r.at[n], dev(y_=yp))
+                send(a_ref.at[:, cols], dst, s1a_s, s1a_r.at[n], dev(y_=yp))
             else:
-                pltpu.make_async_copy(src, dst, s1a_r.at[n]).start()
+                pltpu.make_async_copy(a_hbm.at[:, cols], dst, s1a_r.at[n]).start()
         for r in (1, 2, 3, 7, 6, 5, 4, 0):
             px, pc = xc(r)
-            src = b_ref.at[:, pl.ds(pl.multiple_of(px * 2048 + hb * 1024 + pc * 512 + k * BW, BW), BW)]
+            cols = pl.ds(pl.multiple_of(px * 2048 + hb * 1024 + pc * 512 + k * BW, BW), BW)
             dst = bv.at[n, x, y, c]
             if r:
-                send(src, dst, s1b_s, s1b_r.at[n], dev(x_=px, c_=pc))
+                send(b_ref.at[:, cols], dst, s1b_s, s1b_r.at[n], dev(x_=px, c_=pc))
             else:
-                pltpu.make_async_copy(src, dst, s1b_r.at[n]).start()
+                pltpu.make_async_copy(b_hbm.at[:, cols], dst, s1b_r.at[n]).start()
         return carry
 
     with jax.named_scope("stage1"):
@@ -267,42 +269,44 @@
     HALVES = ((0, pl.ds(0, 128)), (1, pl.ds(128, 128)))
 
     @scoped
-    def multiply_far(m):
-        row(1, m, m, 0, m + 1)
-        column(1, m, 0, 0)
-        for k, cells in parts(m):
-            for h, rows in HALVES:
-                send(psend.at[(1, *cells, rows)], prelay.at[(h, *cells)],
-                     fr_s.at[m, k, h], fr_r.at[m, k, h], (p1, p3)[h])
-
-    def send_1(m, k):
-        for kk, cells in parts(m):
-            if kk == k:
-                send(psend.at[(0, *cells)], precv.at[(0, *cells)], z1_s.at[m, k], z1_r.at[m, k], p1)
-
-    @scoped
-    def row_1(n):
-        row(0, n - 4, n, 1, n - 3)
-        send_1(n - 4, 0)
-
-    @scoped
-    def column_1(n):
-        column(0, n - 4, 4, 1)
-        send_1(n - 4, 1)
-
-    @scoped
-    def multiply_3(n):
-        m = n % 4
-        row(2, m, n, 0, 4)
-        send(psend.at[2, m], precv.at[2, m], z3_s.at[m], z3_r.at[m], p3)
-
-    @scoped
     def pass_on(m):
         for k, cells in parts(m):
             for h, rows in HALVES:
                 src = prelay.at[(h, *cells)]
                 wait(src, fr_r.at[m, k, h])
                 send(src, precv.at[(1, *cells, rows)], ry_s.at[m, k, h], ry_r.at[m, k, h], (p3, p1)[h])
+
+    @scoped
+    def multiply_far(m):
+        row(1, m, m, 0, m + 1)
+        if m:
+            pass_on(m - 1)
+        column(1, m, 0, 0)
+        for k, cells in parts(m):
+            for h, rows in HALVES:
+                send(psend.at[(1, *cells, rows)], prelay.at[(h, *cells)],
+                     fr_s.at[m, k, h], fr_r.at[m, k, h], (p1, p3)[h])
+
+    def send_1(m, k):
+        for kk, cells in parts(m):
+            if kk == k:
+                send(psend.at[(0, *cells)], precv.at[(0, *cells)], z1_s.at[m, k], z1_r.at[m, k], p1)
+
+    @scoped
+    def row_1(n):
+        row(0, n - 4, n, 1, n - 3)
+        send_1(n - 4, 0)
+
+    @scoped
+    def column_1(n):
+        column(0, n - 4, 4, 1)
+        send_1(n - 4, 1)
+
+    @scoped
+    def multiply_3(n):
+        m = n % 4
+        row(2, m, n, 0, 4)
+        send(psend.at[2, m], precv.at[2, m], z3_s.at[m], z3_r.at[m], p3)
 
     row0 = (zl * 4 + y) * 1024
     col0 = ((x * 2 + zh) * 2 + c) * 512
@@ -338,8 +342,6 @@
             row_1(n - 1)
             column_1(n - 1)
             multiply_3(n - 1)
-        if 2 <= n < 5:
-            pass_on(n - 2)
     near_norm(N - 2)
     far(N - 2)
     arrive(N - 1)
@@ -381,26 +383,26 @@
         lax.fori_loop(0, 9, early, 0)
     with jax.named_scope("finish_late"):
         wait(precv.at[2, 3], z3_r.at[3])
-        z1_wait(3)
-
-        def late(t, carry):
-            finish(jnp.where(t < 4, 3, t - 4), jnp.where(t < 4, t, 3))
-            return carry
-
-        lax.fori_loop(0, 7, late, 0)
-
-    lo_mine[0] = jnp.sum(lo_sum[...], 0, keepdims=True)
-    base = 0
-    for k, group in enumerate((plane, zs)):
-        for r, p in enumerate(group):
-            send(lo_mine.at[k], lo_in.at[base + r], lo_s.at[k], lo_r.at[k], p)
-        with jax.named_scope(f"loss_{k}"):
-            wait(lo_in.at[pl.ds(base, len(group))], lo_r.at[k])
-        total = lo_mine[k] + jnp.sum(lo_in[pl.ds(base, len(group))], 0)
-        if k == 0:
-            lo_mine[1] = total
-        base += len(group)
-    loss_ref[0, 0] = jnp.sum(total) / width
+        for k, cells in parts(3):
+            wait(precv.at[(0, *cells)], z1_r.at[3, k])
+
+            def late(t, carry, k=k):
+                finish(*((t, 3) if k else (3, t)))
+                return carry
+
+            lax.fori_loop(0, 4 - k, late, 0)
+
+    lo_mine[...] = jnp.sum(lo_sum[...], 0, keepdims=True)
+    xs, ys4, cs = (x, x1, x2, x3), (y, y1, y2, y3), (c, other)
+    z4 = ((zl, zh), (1 - zl, zh), (zl, 1 - zh), (1 - zl, 1 - zh))
+    steps = [(i, j, k, l) for i in range(4) for j in range(4) for k in range(4) for l in range(2)][1:]
+    far_first = sorted(steps, key=lambda t: -((0, 1, 2, 1)[t[0]] + (0, 1, 2, 1)[t[1]] + (0, 1, 2, 1)[t[2]]))
+    for r, (i, j, k, l) in enumerate(far_first):
+        p = dev(x_=xs[i], y_=ys4[j], c_=cs[l], zl_=z4[k][0], zh_=z4[k][1])
+        send(lo_mine, lo_in.at[r], lo_s, lo_r, p)
+    with jax.named_scope("loss"):
+        wait(lo_in, lo_r)
+    loss_ref[...] = jnp.sum(lo_mine[...] + jnp.sum(lo_in[...], 0), axis=1, keepdims=True) / width
 
     with jax.named_scope("drain"):
         wait(a_ref.at[:, 0:6144], s1a_s)
@@ -424,8 +426,7 @@
         wait(mb_in, mo_s.at[1])
         wait(ma_zin, mo_s.at[2])
         wait(mb_zin, mo_s.at[3])
-        wait(lo_in.at[0:31], lo_s.at[0])
-        wait(lo_in.at[0:3], lo_s.at[1])
+        wait(lo_in, lo_s)
 
 
 def shards(view_a, view_b):
@@ -435,10 +436,11 @@
     vm = pltpu.VMEM
     out, loss = pl.pallas_call(
         lambda *refs: kernel(float(count), float(width), *refs),
-        out_shape=(pltpu.VMEM((1024, 512), F32), jax.ShapeDtypeStruct((1, 1), F32)),
+        out_shape=(pltpu.VMEM((1024, 512), F32), pltpu.VMEM((1, 1), F32)),
         in_specs=[pl.BlockSpec(memory_space=pl.ANY)] * 2,
-        out_specs=(pl.BlockSpec(memory_space=pltpu.VMEM), pl.BlockSpec(memory_space=pltpu.SMEM)),
+        out_specs=(pl.BlockSpec(memory_space=pltpu.VMEM), pl.BlockSpec(memory_space=pltpu.VMEM)),
         scratch_shapes=[
+            vm((S, width), BF16), vm((S, width), BF16), dma((2,)),
             vm((N, 4, 4, 2, S, AW), BF16),
             vm((N, 4, 4, 2, S, BW), BF16),
             vm((N, AW, K), BF16),
@@ -449,16 +451,16 @@
             vm((N, 2, AW), F32), vm((7, N, 2, AW), F32), vm((N, 2, AW), F32), vm((3, N, 2, AW), F32),
             vm((N, 2, BW), F32), vm((3, N, 2, BW), F32), vm((N, 2, BW), F32), vm((3, N, 2, BW), F32),
             vm((N, 2, AW), F32), vm((N, 2, BW), F32),
-            vm((8, 128), F32), vm((2, 1, 128), F32), vm((34, 1, 128), F32),
+            vm((8, 128), F32), vm((1, 128), F32), vm((127, 1, 128), F32),
             dma, dma((N,)), dma, dma((N,)),
             dma((N, 2)), dma((N, 2)), dma((N, 2)), dma((N, 2)), dma((N, 4)), dma((N, 4)),
             dma((N, 2)), dma((N, 2)), dma((N, 2)), dma((N, 2)),
             dma((4, 2)), dma((4, 2)), dma((4,)), dma((4,)),
             dma((4, 2, 2)), dma((4, 2, 2)), dma((4, 2, 2)), dma((4, 2, 2)),
-            dma((4,)), dma((4,)), dma((2,)), dma((2,)),
+            dma((4,)), dma((4,)), dma, dma,
         ],
         compiler_params=pltpu.CompilerParams(
-            collective_id=0, has_side_effects=True, vmem_limit_bytes=56_000_000),
+            collective_id=0, has_side_effects=True, vmem_limit_bytes=59_000_000),
     )(view_a, view_b)
     return out, loss.reshape(())
 

time: 116 us -> 112 us (0.966)
  Pallas kernels: 112 us -> 109 us
    pallas_call x1, Pallas kernels: 112 us -> 109 us  [shards(): pl.pallas_call(lambda *refs: kernel(float(count), float(width), *refs), o...]
where the time goes in v3:
time: 112 us
  Pallas kernels  109 us (97%)
  between operations  1.8 us (2%)
  local copies, waits for them, and re-layouts  1.32 us (1%)
    pallas_call x1, Pallas kernels, shards(): pl.pallas_call(lambda *refs: kernel(float(count), float(width), *refs), o...  109 us

profile of v3, /device:TPU:1, one launch (start us, length us, event | category | flops | bytes accessed | tf_op | source)
XLA Modules:
  0.0 111.8 jit_solution(1090879132772860394)
XLA Ops:
  0.6 108.7 %shard_map.41 = (f32[1024,512]{1,0:T(8,128)S(1)}, f32[1,1]{1,0:T(1,128)S(1)}) custom-call(bf16[96,8192]{1,0:T(8,128)(2,1)} %refs_0_.1, bf16[96,8192]{1,0:T(8,128)(2,1)} %refs_1_.1), custom_call_target="tpu_custom_call" | custom-call | tf_op jit(solution)/shard_map/pallas_call | solution.py:437
  109.3 1.3 %copy.6 = f32[1024,512]{1,0:T(8,128)} copy(f32[1024,512]{1,0:T(8,128)S(1)} %get-tuple-element.6) | data formatting | bytes 4194304

commit v4 on v3

--- a/solution.py
+++ b/solution.py
@@ -22,15 +22,22 @@
 K = 3072
 
 
+def encode(v):
+    return (v * v * (v * jnp.abs(v))).astype(BF16)
+
+
+def decode(v):
+    v = v.astype(F32)
+    root = jnp.sqrt(jnp.sqrt(jnp.abs(v)))
+    return jnp.where(v < 0.0, -root, root)
+
+
 def kernel(count, width, a_hbm, b_hbm, out_ref, loss_ref,
            a_ref, b_ref, in_s, av, bv, at, bn, psend, precv, prelay,
-           ma_mine, ma_in, ma_sum, ma_zin, mb_mine, mb_in, mb_sum, mb_zin, sta, stb,
+           ma_mine, ma_in, ma_sum, mb_mine, mb_in, mb_sum, sta, stb,
            lo_sum, lo_mine, lo_in,
-           s1a_s, s1a_r, s1b_s, s1b_r,
-           aga_s, aga_r, rla_s, rla_r, dd_s, dd_r,
-           agb_s, agb_r, rlb_s, rlb_r,
-           z1_s, z1_r, z3_s, z3_r, fr_s, fr_r, ry_s, ry_r,
-           mo_s, mo_r, lo_s, lo_r):
+           s1a_s, s1a_r, s1b_s, s1b_r, a_s, b_s, z_s, ma_s, mb_s, lo_s,
+           aga_r, rla_r, dd_r, ddf_r, agb_r, rlb_r, z1_r, z3_r, fr_r, mo_r, lo_r):
     zl, y, x, zh, c = (lax.axis_index(n) for n in ROW_COL)
 
     def scoped(f):
@@ -109,16 +116,24 @@
         wait(av.at[n, x, :, c], s1a_r.at[n])
         wait(bv.at[n, :, y], s1b_r.at[n])
 
-    @scoped
-    def own(n, lo=0, hi=4):
-        part = pl.ds(lo, hi - lo)
-        a = av.at[n, x, part, c]
-        send(a, a, aga_s.at[n, 0], aga_r.at[n, 0], dev(x_=x1))
-        send(a, a, aga_s.at[n, 1], aga_r.at[n, 1], dev(x_=x3))
-        b = bv.at[n, part, y]
-        send(b, b, agb_s.at[n, 0], agb_r.at[n, 0], dev(y_=y1))
-        send(b, b, agb_s.at[n, 1], agb_r.at[n, 1], dev(y_=y3))
-        send(a, a, dd_s.at[n, 0], dd_r.at[n, 0], dev(c_=other))
+    def own_part(n, up, down, k):
+        for part, px, py in ((up, x1, y1), (down, x3, y3)):
+            a = av.at[n, x, part, c]
+            send(a, a, a_s, aga_r.at[k], dev(x_=px))
+            b = bv.at[n, part, y]
+            send(b, b, b_s, agb_r.at[k], dev(y_=py))
+
+    ALL, LOW, HIGH = pl.ds(0, 4), pl.ds(0, 2), pl.ds(2, 2)
+
+    @scoped
+    def own(n):
+        if n < N - 1:
+            own_part(n, ALL, ALL, n)
+        else:
+            own_part(n, LOW, HIGH, n)
+            own_part(n, HIGH, LOW, N)
+        a = av.at[n, x, :, c]
+        send(a, a, a_s, dd_r.at[n], dev(c_=other))
 
     def own_moments(n):
         def one(k, acc):
@@ -139,23 +154,38 @@
         mb_mine[n, 0:1, :] = jnp.sum(sb, 0, keepdims=True)
         mb_mine[n, 1:2, :] = jnp.sum(qb, 0, keepdims=True)
 
+    def relay(n):
+        for v, part, px in ((x3, LOW, x1), (x1, HIGH, x3)):
+            a = av.at[n, v, part, c]
+            send(a, a, a_s, rla_r.at[n], dev(x_=px))
+        for v, part, py in ((y3, LOW, y1), (y1, HIGH, y3)):
+            b = bv.at[n, part, v]
+            send(b, b, b_s, rlb_r.at[n], dev(y_=py))
+
+    def share(n, part3, part1):
+        for v, part in ((x3, part3), (x1, part1)):
+            a = av.at[n, v, part, c]
+            send(a, a, a_s, dd_r.at[n], dev(c_=other))
+
     @scoped
     def arrive(n):
-        wait(av.at[n, x3, :, c], aga_r.at[n, 0])
-        a = av.at[n, x3, 0:2, c]
-        send(a, a, rla_s.at[n, 0], rla_r.at[n, 0], dev(x_=x1))
-        wait(av.at[n, x1, :, c], aga_r.at[n, 1])
-        a = av.at[n, x1, 2:4, c]
-        send(a, a, rla_s.at[n, 1], rla_r.at[n, 1], dev(x_=x3))
-        wait(bv.at[n, :, y3], agb_r.at[n, 0])
-        b = bv.at[n, 0:2, y3]
-        send(b, b, rlb_s.at[n, 0], rlb_r.at[n, 0], dev(y_=y1))
-        wait(bv.at[n, :, y1], agb_r.at[n, 1])
-        b = bv.at[n, 2:4, y1]
-        send(b, b, rlb_s.at[n, 1], rlb_r.at[n, 1], dev(y_=y3))
-        for k, v in ((1, x3), (2, x1)):
-            a = av.at[n, v, :, c]
-            send(a, a, dd_s.at[n, k], dd_r.at[n, k], dev(c_=other))
+        wait(av.at[n, 0:2, :, c], aga_r.at[n])
+        wait(bv.at[n, :, 0:2], agb_r.at[n])
+        relay(n)
+        share(n, ALL, ALL)
+
+    @scoped
+    def arrive_first(n):
+        wait(av.at[n, 0, :, c], aga_r.at[n])
+        wait(bv.at[n, :, 0], agb_r.at[n])
+        relay(n)
+        share(n, LOW, HIGH)
+
+    @scoped
+    def arrive_second(n):
+        wait(av.at[n, 0, :, c], aga_r.at[n + 1])
+        wait(bv.at[n, :, 0], agb_r.at[n + 1])
+        share(n, HIGH, LOW)
 
     def wait_and_sum(n, carry):
         s1_wait(n)
@@ -168,30 +198,31 @@
         own_moments(0)
         lax.fori_loop(1, N, wait_and_sum, 0)
     for r, p in enumerate(xcs):
-        send(ma_mine, ma_in.at[r], mo_s.at[0], mo_r.at[0], p)
+        send(ma_mine, ma_in.at[r], ma_s, mo_r.at[0], p)
     for r, p in enumerate(ys):
-        send(mb_mine, mb_in.at[r], mo_s.at[1], mo_r.at[1], p)
+        send(mb_mine, mb_in.at[r], mb_s, mo_r.at[1], p)
     own(1)
     arrive(0)
     own(2)
     with jax.named_scope("mom_1"):
-        wait(ma_in, mo_r.at[0])
-        wait(mb_in, mo_r.at[1])
-    ma_sum[...] = ma_mine[...] + jnp.sum(ma_in[...], 0)
-    mb_sum[...] = mb_mine[...] + jnp.sum(mb_in[...], 0)
+        wait(ma_in.at[0:7], mo_r.at[0])
+        wait(mb_in.at[0:3], mo_r.at[1])
+    ma_sum[...] = ma_mine[...] + jnp.sum(ma_in[0:7], 0)
+    mb_sum[...] = mb_mine[...] + jnp.sum(mb_in[0:3], 0)
     for r, p in enumerate(zs):
-        send(ma_sum, ma_zin.at[r], mo_s.at[2], mo_r.at[2], p)
-        send(mb_sum, mb_zin.at[r], mo_s.at[3], mo_r.at[3], p)
+        send(ma_sum, ma_in.at[7 + r], ma_s, mo_r.at[2], p)
+        send(mb_sum, mb_in.at[3 + r], mb_s, mo_r.at[3], p)
     arrive(1)
     own(3)
 
     def moments_done():
         with jax.named_scope("mom_2"):
-            wait(ma_zin, mo_r.at[2])
-            wait(mb_zin, mo_r.at[3])
-        for mine, zin, st, turn in ((ma_sum, ma_zin, sta, (4, 0, 4)), (mb_sum, mb_zin, stb, (0, 4, 4))):
+            wait(ma_in.at[7:10], mo_r.at[2])
+            wait(mb_in.at[3:6], mo_r.at[3])
+        for mine, zin, z0, st, turn in ((ma_sum, ma_in, 7, sta, (4, 0, 4)), (mb_sum, mb_in, 3, stb, (0, 4, 4))):
             for n in range(N):
-                total = mine[n] + zin[0, (n + turn[0]) % N] + zin[1, (n + turn[1]) % N] + zin[2, (n + turn[2]) % N]
+                total = (mine[n] + zin[z0, (n + turn[0]) % N] + zin[z0 + 1, (n + turn[1]) % N]
+                         + zin[z0 + 2, (n + turn[2]) % N])
                 mean = total[0:1, :] / count
                 var = total[1:2, :] / count - mean * mean
                 st[n, 0:1, :] = mean
@@ -199,12 +230,10 @@
 
     @scoped
     def far(n):
-        wait(av.at[n, x2, 0:2, c], rla_r.at[n, 0])
-        wait(av.at[n, x2, 2:4, c], rla_r.at[n, 1])
+        wait(av.at[n, x2, :, c], rla_r.at[n])
         a = av.at[n, x2, :, c]
-        send(a, a, dd_s.at[n, 3], dd_r.at[n, 3], dev(c_=other))
-        wait(bv.at[n, 0:2, y2], rlb_r.at[n, 0])
-        wait(bv.at[n, 2:4, y2], rlb_r.at[n, 1])
+        send(a, a, a_s, ddf_r.at[n], dev(c_=other))
+        wait(bv.at[n, :, y2], rlb_r.at[n])
 
     def norm_a(n, lo, hi):
         def group(g, carry):
@@ -234,14 +263,13 @@
 
     @scoped
     def near_norm(n):
-        for k, v in ((0, x), (1, x3), (2, x1)):
-            wait(av.at[n, v, :, other], dd_r.at[n, k])
+        wait(av.at[n, 0:3, :, other], dd_r.at[n])
         norm_a(n, 0, 6)
         norm_b(n, 0, 4)
 
     @scoped
     def far_norm(n):
-        wait(av.at[n, x2, :, other], dd_r.at[n, 3])
+        wait(av.at[n, x2, :, other], ddf_r.at[n])
         norm_a(n, 6, 8)
         norm_b(n, 4, 8)
 
@@ -249,17 +277,30 @@
         r = jnp.dot(at[i], bn[half, :, j * BW:(j + n) * BW], preferred_element_type=F32)
         return r * (1.0 / count)
 
+    def keep(slot, i, j, v):
+        if slot == 1:
+            psend[slot, i, j] = encode(v)
+        elif slot == 0:
+            psend[slot, i, j, 0:128] = encode(v[0:128])
+            psend[slot, i, j, 128:256] = encode(v[128:256] + decode(prelay[1, i, j]))
+        else:
+            psend[slot, i, j, 0:128] = encode(v[0:128] + decode(prelay[0, i, j]))
+            psend[slot, i, j, 128:256] = encode(v[128:256])
+
     def row(slot, m, i, half, n):
         r = dot(i, half, 0, n)
         for j in range(n):
-            psend[slot, m, j] = r[:, j * BW:(j + 1) * BW].astype(BF16)
+            keep(slot, m, j, r[:, j * BW:(j + 1) * BW])
 
     def column(slot, m, base, half):
         def one(i, carry):
-            psend[slot, i, m] = dot(base + i, half, m, 1).astype(BF16)
+            keep(slot, i, m, dot(base + i, half, m, 1))
             return carry
 
         lax.fori_loop(0, m, one, 0)
+
+    def far_wait(m, h):
+        wait(bn.at[0, pl.ds(0, 32 * (2 * m + 1))], fr_r.at[m, h])
 
     def parts(m):
         yield 0, (m, pl.ds(0, m + 1))
@@ -269,31 +310,22 @@
     HALVES = ((0, pl.ds(0, 128)), (1, pl.ds(128, 128)))
 
     @scoped
-    def pass_on(m):
-        for k, cells in parts(m):
-            for h, rows in HALVES:
-                src = prelay.at[(h, *cells)]
-                wait(src, fr_r.at[m, k, h])
-                send(src, precv.at[(1, *cells, rows)], ry_s.at[m, k, h], ry_r.at[m, k, h], (p3, p1)[h])
-
-    @scoped
     def multiply_far(m):
         row(1, m, m, 0, m + 1)
-        if m:
-            pass_on(m - 1)
         column(1, m, 0, 0)
         for k, cells in parts(m):
             for h, rows in HALVES:
                 send(psend.at[(1, *cells, rows)], prelay.at[(h, *cells)],
-                     fr_s.at[m, k, h], fr_r.at[m, k, h], (p1, p3)[h])
+                     z_s, fr_r.at[m, h], (p1, p3)[h])
 
     def send_1(m, k):
         for kk, cells in parts(m):
             if kk == k:
-                send(psend.at[(0, *cells)], precv.at[(0, *cells)], z1_s.at[m, k], z1_r.at[m, k], p1)
+                send(psend.at[(0, *cells)], precv.at[(0, *cells)], z_s, z1_r.at[k + 1 if m == 3 else 0], p1)
 
     @scoped
     def row_1(n):
+        far_wait(n - 4, 1)
         row(0, n - 4, n, 1, n - 3)
         send_1(n - 4, 0)
 
@@ -304,16 +336,19 @@
 
     @scoped
     def multiply_3(n):
-        m = n % 4
+        m = n - 4
+        if m == 0:
+            for k in range(4):
+                far_wait(k, 0)
         row(2, m, n, 0, 4)
-        send(psend.at[2, m], precv.at[2, m], z3_s.at[m], z3_r.at[m], p3)
+        send(psend.at[2, m], precv.at[1, m], z_s, z3_r.at[m // 3], p3)
 
     row0 = (zl * 4 + y) * 1024
     col0 = ((x * 2 + zh) * 2 + c) * 512
 
     def finish(i, j):
         at_ = (pl.ds(pl.multiple_of(i * AW, AW), AW), pl.ds(pl.multiple_of(j * BW, BW), BW))
-        v = out_ref[at_] + precv[1, i, j].astype(F32) + precv[2, i, j].astype(F32) + precv[0, i, j].astype(F32)
+        v = out_ref[at_] + (decode(precv[0, i, j]) + decode(precv[1, i, j]))
         out_ref[at_] = v
         rows = row0 + i * AW + lax.broadcasted_iota(jnp.int32, (AW, BW), 0)
         cols = col0 + j * BW + lax.broadcasted_iota(jnp.int32, (AW, BW), 1)
@@ -327,31 +362,30 @@
             arrive(n)
             if n + 2 < N - 1:
                 own(n + 2)
-            elif n + 2 == N - 1:
-                own(N - 1, 0, 2)
-            else:
-                own(N - 1, 2, 4)
+            elif n + 1 == N - 1:
+                own(N - 1)
         near_norm(n - 1)
+        if n == N - 2:
+            multiply_3(4)
         far(n - 1)
-        if n == 6:
-            pass_on(3)
         far_norm(n - 1)
         if n < 5:
             multiply_far(n - 1)
         else:
             row_1(n - 1)
             column_1(n - 1)
-            multiply_3(n - 1)
     near_norm(N - 2)
     far(N - 2)
-    arrive(N - 1)
+    arrive_first(N - 1)
+    multiply_3(5)
     far_norm(N - 2)
     row_1(N - 2)
-    far(N - 1)
+    arrive_second(N - 1)
     column_1(N - 2)
     near_norm(N - 1)
+    far(N - 1)
+    multiply_3(6)
     far_norm(N - 1)
-    multiply_3(N - 2)
     row_1(N - 1)
     column_1(N - 1)
     multiply_3(N - 1)
@@ -363,18 +397,9 @@
 
         lax.fori_loop(0, 4, mine, 0)
 
-    def z1_wait(m):
-        for k, cells in parts(m):
-            wait(precv.at[(0, *cells)], z1_r.at[m, k])
-
     with jax.named_scope("finish_early"):
-        for m in range(4):
-            for k, cells in parts(m):
-                for h, rows in HALVES:
-                    wait(precv.at[(1, *cells, rows)], ry_r.at[m, k, h])
-        for m in range(3):
-            wait(precv.at[2, m], z3_r.at[m])
-            z1_wait(m)
+        wait(precv.at[1, 0:3], z3_r.at[0])
+        wait(precv.at[0, 0:3, 0:3], z1_r.at[0])
 
         def early(t, carry):
             finish(lax.div(t, 3), lax.rem(t, 3))
@@ -382,9 +407,9 @@
 
         lax.fori_loop(0, 9, early, 0)
     with jax.named_scope("finish_late"):
-        wait(precv.at[2, 3], z3_r.at[3])
+        wait(precv.at[1, 3], z3_r.at[1])
         for k, cells in parts(3):
-            wait(precv.at[(0, *cells)], z1_r.at[3, k])
+            wait(precv.at[(0, *cells)], z1_r.at[k + 1])
 
             def late(t, carry, k=k):
                 finish(*((t, 3) if k else (3, t)))
@@ -407,25 +432,11 @@
     with jax.named_scope("drain"):
         wait(a_ref.at[:, 0:6144], s1a_s)
         wait(b_ref.at[:, 0:7168], s1b_s)
-        for n in range(N):
-            for k in range(2):
-                wait(av.at[n, x, :, c], aga_s.at[n, k])
-                wait(bv.at[n, :, y], agb_s.at[n, k])
-                wait(av.at[n, x, 0:2, c], rla_s.at[n, k])
-                wait(bv.at[n, 0:2, y], rlb_s.at[n, k])
-            for k in range(4):
-                wait(av.at[n, x, :, c], dd_s.at[n, k])
-        for m in range(4):
-            for k, cells in parts(m):
-                wait(precv.at[(0, *cells)], z1_s.at[m, k])
-                for h, rows in HALVES:
-                    wait(prelay.at[(h, *cells)], fr_s.at[m, k, h])
-                    wait(prelay.at[(h, *cells)], ry_s.at[m, k, h])
-            wait(precv.at[2, m], z3_s.at[m])
-        wait(ma_in, mo_s.at[0])
-        wait(mb_in, mo_s.at[1])
-        wait(ma_zin, mo_s.at[2])
-        wait(mb_zin, mo_s.at[3])
+        wait(av.at[0:7], a_s)
+        wait(bv.at[0:6], b_s)
+        wait(psend, z_s)
+        wait(ma_in, ma_s)
+        wait(mb_in, mb_s)
         wait(lo_in, lo_s)
 
 
@@ -446,18 +457,15 @@
             vm((N, AW, K), BF16),
             vm((2, K, 4 * BW), BF16),
             vm((3, 4, 4, AW, BW), BF16),
-            vm((3, 4, 4, AW, BW), BF16),
+            vm((2, 4, 4, AW, BW), BF16),
             vm((2, 4, 4, AW // 2, BW), BF16),
-            vm((N, 2, AW), F32), vm((7, N, 2, AW), F32), vm((N, 2, AW), F32), vm((3, N, 2, AW), F32),
-            vm((N, 2, BW), F32), vm((3, N, 2, BW), F32), vm((N, 2, BW), F32), vm((3, N, 2, BW), F32),
+            vm((N, 2, AW), F32), vm((10, N, 2, AW), F32), vm((N, 2, AW), F32),
+            vm((N, 2, BW), F32), vm((6, N, 2, BW), F32), vm((N, 2, BW), F32),
             vm((N, 2, AW), F32), vm((N, 2, BW), F32),
             vm((8, 128), F32), vm((1, 128), F32), vm((127, 1, 128), F32),
-            dma, dma((N,)), dma, dma((N,)),
-            dma((N, 2)), dma((N, 2)), dma((N, 2)), dma((N, 2)), dma((N, 4)), dma((N, 4)),
-            dma((N, 2)), dma((N, 2)), dma((N, 2)), dma((N, 2)),
-            dma((4, 2)), dma((4, 2)), dma((4,)), dma((4,)),
-            dma((4, 2, 2)), dma((4, 2, 2)), dma((4, 2, 2)), dma((4, 2, 2)),
-            dma((4,)), dma((4,)), dma, dma,
+            dma, dma((N,)), dma, dma((N,)), dma, dma, dma, dma, dma, dma,
+            dma((N + 1,)), dma((N,)), dma((N,)), dma((N,)), dma((N + 1,)), dma((N,)),
+            dma((3,)), dma((2,)), dma((4, 2)), dma((4,)), dma,
         ],
         compiler_params=pltpu.CompilerParams(
             collective_id=0, has_side_effects=True, vmem_limit_bytes=59_000_000),

time: 112 us -> 108 us (0.964)
  Pallas kernels: 109 us -> 105 us
    pallas_call x1, Pallas kernels: 109 us -> 105 us  [shards(): pl.pallas_call(lambda *refs: kernel(float(count), float(width), *refs), o...]
where the time goes in v4:
time: 108 us
  Pallas kernels  105 us (97%)
  between operations  1.8 us (2%)
  local copies, waits for them, and re-layouts  1.32 us (1%)
    pallas_call x1, Pallas kernels, shards(): pl.pallas_call(lambda *refs: kernel(float(count), float(width), *refs), o...  105 us

profile of v4, /device:TPU:1, one launch (start us, length us, event | category | flops | bytes accessed | tf_op | source)
XLA Modules:
  0.0 107.8 jit_solution(3424505644771497401)
XLA Ops:
  0.6 104.6 %shard_map.41 = (f32[1024,512]{1,0:T(8,128)S(1)}, f32[1,1]{1,0:T(1,128)S(1)}) custom-call(bf16[96,8192]{1,0:T(8,128)(2,1)} %refs_0_.1, bf16[96,8192]{1,0:T(8,128)(2,1)} %refs_1_.1), custom_call_target="tpu_custom_call" | custom-call | tf_op jit(solution)/shard_map/pallas_call | solution.py:448
  105.3 1.3 %copy.6 = f32[1024,512]{1,0:T(8,128)} copy(f32[1024,512]{1,0:T(8,128)S(1)} %get-tuple-element.6) | data formatting | bytes 4194304

commit v5 on v4

--- a/solution.py
+++ b/solution.py
@@ -34,8 +34,8 @@
 
 def kernel(count, width, a_hbm, b_hbm, out_ref, loss_ref,
            a_ref, b_ref, in_s, av, bv, at, bn, psend, precv, prelay,
-           ma_mine, ma_in, ma_sum, mb_mine, mb_in, mb_sum, sta, stb,
-           lo_sum, lo_mine, lo_in,
+           ma_mine, ma_in, ma_sum, ma_all, mb_mine, mb_in, mb_sum, sta, stb,
+           held, lo_sum, lo_mine, lo_in,
            s1a_s, s1a_r, s1b_s, s1b_r, a_s, b_s, z_s, ma_s, mb_s, lo_s,
            aga_r, rla_r, dd_r, ddf_r, agb_r, rlb_r, z1_r, z3_r, fr_r, mo_r, lo_r):
     zl, y, x, zh, c = (lax.axis_index(n) for n in ROW_COL)
@@ -197,29 +197,33 @@
         own(0)
         own_moments(0)
         lax.fori_loop(1, N, wait_and_sum, 0)
-    for r, p in enumerate(xcs):
-        send(ma_mine, ma_in.at[r], ma_s, mo_r.at[0], p)
+    send(ma_mine, ma_in.at[6], ma_s, mo_r.at[4], dev(c_=other))
+    with jax.named_scope("mom_0"):
+        wait(ma_in.at[6], mo_r.at[4])
+    ma_sum[...] = ma_mine[...] + ma_in[6]
+    for r, v in enumerate((x1, x2, x3)):
+        send(ma_sum, ma_in.at[r], ma_s, mo_r.at[0], dev(x_=v))
     for r, p in enumerate(ys):
         send(mb_mine, mb_in.at[r], mb_s, mo_r.at[1], p)
     own(1)
     arrive(0)
     own(2)
     with jax.named_scope("mom_1"):
-        wait(ma_in.at[0:7], mo_r.at[0])
+        wait(ma_in.at[0:3], mo_r.at[0])
         wait(mb_in.at[0:3], mo_r.at[1])
-    ma_sum[...] = ma_mine[...] + jnp.sum(ma_in[0:7], 0)
+    ma_all[...] = ma_sum[...] + jnp.sum(ma_in[0:3], 0)
     mb_sum[...] = mb_mine[...] + jnp.sum(mb_in[0:3], 0)
     for r, p in enumerate(zs):
-        send(ma_sum, ma_in.at[7 + r], ma_s, mo_r.at[2], p)
+        send(ma_all, ma_in.at[3 + r], ma_s, mo_r.at[2], p)
         send(mb_sum, mb_in.at[3 + r], mb_s, mo_r.at[3], p)
     arrive(1)
     own(3)
 
     def moments_done():
         with jax.named_scope("mom_2"):
-            wait(ma_in.at[7:10], mo_r.at[2])
+            wait(ma_in.at[3:6], mo_r.at[2])
             wait(mb_in.at[3:6], mo_r.at[3])
-        for mine, zin, z0, st, turn in ((ma_sum, ma_in, 7, sta, (4, 0, 4)), (mb_sum, mb_in, 3, stb, (0, 4, 4))):
+        for mine, zin, z0, st, turn in ((ma_all, ma_in, 3, sta, (4, 0, 4)), (mb_sum, mb_in, 3, stb, (0, 4, 4))):
             for n in range(N):
                 total = (mine[n] + zin[z0, (n + turn[0]) % N] + zin[z0 + 1, (n + turn[1]) % N]
                          + zin[z0 + 2, (n + turn[2]) % N])
@@ -311,28 +315,43 @@
 
     @scoped
     def multiply_far(m):
-        row(1, m, m, 0, m + 1)
-        column(1, m, 0, 0)
         for k, cells in parts(m):
+            if k:
+                column(1, m, 0, 0)
+            else:
+                row(1, m, m, 0, m + 1)
             for h, rows in HALVES:
                 send(psend.at[(1, *cells, rows)], prelay.at[(h, *cells)],
                      z_s, fr_r.at[m, h], (p1, p3)[h])
 
-    def send_1(m, k):
-        for kk, cells in parts(m):
-            if kk == k:
-                send(psend.at[(0, *cells)], precv.at[(0, *cells)], z_s, z1_r.at[k + 1 if m == 3 else 0], p1)
+    def send_1(cells, k):
+        send(psend.at[(0, *cells)], precv.at[(0, *cells)], z_s, z1_r.at[k], p1)
 
     @scoped
     def row_1(n):
-        far_wait(n - 4, 1)
-        row(0, n - 4, n, 1, n - 3)
-        send_1(n - 4, 0)
+        m = n - 4
+        far_wait(m, 1)
+        r = dot(n, 1, 0, m + 1)
+        for j in range(m + 1):
+            keep(0, m, j, r[:, j * BW:(j + 1) * BW])
+            if m == 3:
+                send_1((m, j), 1 + j)
+        if m < 3:
+            send_1((m, pl.ds(0, m + 1)), 0)
 
     @scoped
     def column_1(n):
-        column(0, n - 4, 4, 1)
-        send_1(n - 4, 1)
+        m = n - 4
+
+        def one(i, carry):
+            keep(0, i, m, dot(4 + i, 1, m, 1))
+            if m == 3:
+                send_1((i, m), 5 + i)
+            return carry
+
+        lax.fori_loop(0, m, one, 0)
+        if 0 < m < 3:
+            send_1((pl.ds(0, m), m), 0)
 
     @scoped
     def multiply_3(n):
@@ -340,15 +359,28 @@
         if m == 0:
             for k in range(4):
                 far_wait(k, 0)
-        row(2, m, n, 0, 4)
-        send(psend.at[2, m], precv.at[1, m], z_s, z3_r.at[m // 3], p3)
+            r = held[...]
+        else:
+            r = dot(n, 0, 0, 4)
+        for j in range(4):
+            keep(2, m, j, r[:, j * BW:(j + 1) * BW])
+            if m == 3:
+                send(psend.at[2, m, j], precv.at[1, m, j], z_s, z3_r.at[1 + j], p3)
+        if m < 3:
+            send(psend.at[2, m], precv.at[1, m], z_s, z3_r.at[0], p3)
 
     row0 = (zl * 4 + y) * 1024
     col0 = ((x * 2 + zh) * 2 + c) * 512
 
-    def finish(i, j):
-        at_ = (pl.ds(pl.multiple_of(i * AW, AW), AW), pl.ds(pl.multiple_of(j * BW, BW), BW))
-        v = out_ref[at_] + (decode(precv[0, i, j]) + decode(precv[1, i, j]))
+    def spot(i, j):
+        return pl.ds(pl.multiple_of(i * AW, AW), AW), pl.ds(pl.multiple_of(j * BW, BW), BW)
+
+    def add(slot, i, j):
+        out_ref[spot(i, j)] = out_ref[spot(i, j)] + decode(precv[slot, i, j])
+
+    def finish(slot, i, j):
+        at_ = spot(i, j)
+        v = out_ref[at_] + decode(precv[slot, i, j])
         out_ref[at_] = v
         rows = row0 + i * AW + lax.broadcasted_iota(jnp.int32, (AW, BW), 0)
         cols = col0 + j * BW + lax.broadcasted_iota(jnp.int32, (AW, BW), 1)
@@ -365,30 +397,32 @@
             elif n + 1 == N - 1:
                 own(N - 1)
         near_norm(n - 1)
+        far(n - 1)
         if n == N - 2:
             multiply_3(4)
-        far(n - 1)
+            near_norm(6)
         far_norm(n - 1)
         if n < 5:
             multiply_far(n - 1)
-        else:
-            row_1(n - 1)
-            column_1(n - 1)
-    near_norm(N - 2)
-    far(N - 2)
-    arrive_first(N - 1)
+        if n == 5:
+            row_1(4)
+            held[...] = dot(4, 0, 0, 4)
+    row_1(5)
+    far(6)
+    column_1(5)
     multiply_3(5)
-    far_norm(N - 2)
-    row_1(N - 2)
-    arrive_second(N - 1)
-    column_1(N - 2)
-    near_norm(N - 1)
-    far(N - 1)
+    arrive_first(7)
+    far_norm(6)
+    row_1(6)
+    arrive_second(7)
+    column_1(6)
     multiply_3(6)
-    far_norm(N - 1)
-    row_1(N - 1)
-    column_1(N - 1)
-    multiply_3(N - 1)
+    far(7)
+    near_norm(7)
+    far_norm(7)
+    row_1(7)
+    column_1(7)
+    multiply_3(7)
 
     with jax.named_scope("mine"):
         def mine(i, carry):
@@ -399,23 +433,40 @@
 
     with jax.named_scope("finish_early"):
         wait(precv.at[1, 0:3], z3_r.at[0])
+
+        def adds(t, carry):
+            add(1, lax.div(t, 4), lax.rem(t, 4))
+            return carry
+
+        lax.fori_loop(0, 12, adds, 0)
         wait(precv.at[0, 0:3, 0:3], z1_r.at[0])
 
         def early(t, carry):
-            finish(lax.div(t, 3), lax.rem(t, 3))
+            finish(0, lax.div(t, 3), lax.rem(t, 3))
             return carry
 
         lax.fori_loop(0, 9, early, 0)
     with jax.named_scope("finish_late"):
-        wait(precv.at[1, 3], z3_r.at[1])
-        for k, cells in parts(3):
-            wait(precv.at[(0, *cells)], z1_r.at[k + 1])
-
-            def late(t, carry, k=k):
-                finish(*((t, 3) if k else (3, t)))
-                return carry
-
-            lax.fori_loop(0, 4 - k, late, 0)
+        def late_row(t, carry):
+            wait(precv.at[0, 3, t], z1_r.at[1 + t])
+            add(0, 3, t)
+            return carry
+
+        def late_3(t, carry):
+            wait(precv.at[1, 3, t], z3_r.at[1 + t])
+            finish(1, 3, t)
+            return carry
+
+        def late_column(t, carry):
+            wait(precv.at[0, t, 3], z1_r.at[5 + t])
+            finish(0, t, 3)
+            return carry
+
+        lax.fori_loop(0, 4, late_row, 0)
+        with jax.named_scope("late_3"):
+            lax.fori_loop(0, 4, late_3, 0)
+        with jax.named_scope("late_1"):
+            lax.fori_loop(0, 3, late_column, 0)
 
     lo_mine[...] = jnp.sum(lo_sum[...], 0, keepdims=True)
     xs, ys4, cs = (x, x1, x2, x3), (y, y1, y2, y3), (c, other)
@@ -459,13 +510,14 @@
             vm((3, 4, 4, AW, BW), BF16),
             vm((2, 4, 4, AW, BW), BF16),
             vm((2, 4, 4, AW // 2, BW), BF16),
-            vm((N, 2, AW), F32), vm((10, N, 2, AW), F32), vm((N, 2, AW), F32),
+            vm((N, 2, AW), F32), vm((7, N, 2, AW), F32), vm((N, 2, AW), F32), vm((N, 2, AW), F32),
             vm((N, 2, BW), F32), vm((6, N, 2, BW), F32), vm((N, 2, BW), F32),
             vm((N, 2, AW), F32), vm((N, 2, BW), F32),
+            vm((AW, 4 * BW), F32),
             vm((8, 128), F32), vm((1, 128), F32), vm((127, 1, 128), F32),
             dma, dma((N,)), dma, dma((N,)), dma, dma, dma, dma, dma, dma,
             dma((N + 1,)), dma((N,)), dma((N,)), dma((N,)), dma((N + 1,)), dma((N,)),
-            dma((3,)), dma((2,)), dma((4, 2)), dma((4,)), dma,
+            dma((8,)), dma((5,)), dma((4, 2)), dma((5,)), dma,
         ],
         compiler_params=pltpu.CompilerParams(
             collective_id=0, has_side_effects=True, vmem_limit_bytes=59_000_000),

time: 108 us -> 106 us (0.981)
  Pallas kernels: 105 us -> 103 us
    pallas_call x1, Pallas kernels: 105 us -> 103 us  [shards(): pl.pallas_call(lambda *refs: kernel(float(count), float(width), *refs), o...]
where the time goes in v5:
time: 106 us
  Pallas kernels  103 us (97%)
  between operations  1.8 us (2%)
  local copies, waits for them, and re-layouts  1.32 us (1%)
    pallas_call x1, Pallas kernels, shards(): pl.pallas_call(lambda *refs: kernel(float(count), float(width), *refs), o...  103 us

profile of v5, /device:TPU:1, one launch (start us, length us, event | category | flops | bytes accessed | tf_op | source)
XLA Modules:
  0.0 106.0 jit_solution(7157257319943947483)
XLA Ops:
  0.6 102.9 %shard_map.41 = (f32[1024,512]{1,0:T(8,128)S(1)}, f32[1,1]{1,0:T(1,128)S(1)}) custom-call(bf16[96,8192]{1,0:T(8,128)(2,1)} %refs_0_.1, bf16[96,8192]{1,0:T(8,128)(2,1)} %refs_1_.1), custom_call_target="tpu_custom_call" | custom-call | tf_op jit(solution)/shard_map/pallas_call | solution.py:499
  103.6 1.3 %copy.6 = f32[1024,512]{1,0:T(8,128)} copy(f32[1024,512]{1,0:T(8,128)S(1)} %get-tuple-element.6) | data formatting | bytes 4194304

commit v6 on v5

--- a/solution.py
+++ b/solution.py
@@ -272,10 +272,13 @@
         norm_b(n, 0, 4)
 
     @scoped
-    def far_norm(n):
+    def far_norm_b(n):
+        norm_b(n, 4, 8)
+
+    @scoped
+    def far_norm_a(n):
         wait(av.at[n, x2, :, other], ddf_r.at[n])
         norm_a(n, 6, 8)
-        norm_b(n, 4, 8)
 
     def dot(i, half, j, n):
         r = jnp.dot(at[i], bn[half, :, j * BW:(j + n) * BW], preferred_element_type=F32)
@@ -330,7 +333,8 @@
     @scoped
     def row_1(n):
         m = n - 4
-        far_wait(m, 1)
+        if m == 0:
+            far_wait(0, 1)
         r = dot(n, 1, 0, m + 1)
         for j in range(m + 1):
             keep(0, m, j, r[:, j * BW:(j + 1) * BW])
@@ -342,6 +346,9 @@
     @scoped
     def column_1(n):
         m = n - 4
+
+        if m:
+            far_wait(m, 1)
 
         def one(i, carry):
             keep(0, i, m, dot(4 + i, 1, m, 1))
@@ -389,39 +396,45 @@
 
     lo_sum[...] = jnp.zeros_like(lo_sum)
     moments_done()
-    for n in range(1, N - 1):
+    for n in range(1, N - 2):
         if n > 1:
             arrive(n)
             if n + 2 < N - 1:
                 own(n + 2)
-            elif n + 1 == N - 1:
-                own(N - 1)
         near_norm(n - 1)
         far(n - 1)
-        if n == N - 2:
-            multiply_3(4)
-            near_norm(6)
-        far_norm(n - 1)
+        far_norm_b(n - 1)
+        far_norm_a(n - 1)
         if n < 5:
             multiply_far(n - 1)
-        if n == 5:
+        else:
             row_1(4)
             held[...] = dot(4, 0, 0, 4)
+    arrive(6)
+    own(7)
+    near_norm(5)
+    far(5)
+    multiply_3(4)
+    far_norm_b(5)
+    column_1(5)
+    far_norm_a(5)
     row_1(5)
+    near_norm(6)
     far(6)
-    column_1(5)
+    far_norm_b(6)
+    column_1(6)
     multiply_3(5)
     arrive_first(7)
-    far_norm(6)
+    far_norm_a(6)
     row_1(6)
     arrive_second(7)
-    column_1(6)
     multiply_3(6)
+    near_norm(7)
     far(7)
-    near_norm(7)
-    far_norm(7)
+    far_norm_b(7)
+    column_1(7)
+    far_norm_a(7)
     row_1(7)
-    column_1(7)
     multiply_3(7)
 
     with jax.named_scope("mine"):
@@ -447,26 +460,22 @@
 
         lax.fori_loop(0, 9, early, 0)
     with jax.named_scope("finish_late"):
+        def late_column(t, carry):
+            wait(precv.at[0, t, 3], z1_r.at[5 + t])
+            finish(0, t, 3)
+            return carry
+
         def late_row(t, carry):
             wait(precv.at[0, 3, t], z1_r.at[1 + t])
             add(0, 3, t)
-            return carry
-
-        def late_3(t, carry):
             wait(precv.at[1, 3, t], z3_r.at[1 + t])
             finish(1, 3, t)
             return carry
 
-        def late_column(t, carry):
-            wait(precv.at[0, t, 3], z1_r.at[5 + t])
-            finish(0, t, 3)
-            return carry
-
-        lax.fori_loop(0, 4, late_row, 0)
-        with jax.named_scope("late_3"):
-            lax.fori_loop(0, 4, late_3, 0)
-        with jax.named_scope("late_1"):
+        with jax.named_scope("late_column"):
             lax.fori_loop(0, 3, late_column, 0)
+        with jax.named_scope("late_row"):
+            lax.fori_loop(0, 4, late_row, 0)
 
     lo_mine[...] = jnp.sum(lo_sum[...], 0, keepdims=True)
     xs, ys4, cs = (x, x1, x2, x3), (y, y1, y2, y3), (c, other)

time: 106 us -> 105 us (level)
  no operation moved by 1% of the time
where the time goes in v6:
time: 105 us
  Pallas kernels  102 us (97%)
  between operations  1.8 us (2%)
  local copies, waits for them, and re-layouts  1.32 us (1%)
    pallas_call x1, Pallas kernels, shards(): pl.pallas_call(lambda *refs: kernel(float(count), float(width), *refs), o...  102 us

profile of v6, /device:TPU:1, one launch (start us, length us, event | category | flops | bytes accessed | tf_op | source)
XLA Modules:
  0.0 105.0 jit_solution(11260032757966043850)
XLA Ops:
  0.6 101.9 %shard_map.41 = (f32[1024,512]{1,0:T(8,128)S(1)}, f32[1,1]{1,0:T(1,128)S(1)}) custom-call(bf16[96,8192]{1,0:T(8,128)(2,1)} %refs_0_.1, bf16[96,8192]{1,0:T(8,128)(2,1)} %refs_1_.1), custom_call_target="tpu_custom_call" | custom-call | tf_op jit(solution)/shard_map/pallas_call | solution.py:508
  102.5 1.3 %copy.6 = f32[1024,512]{1,0:T(8,128)} copy(f32[1024,512]{1,0:T(8,128)S(1)} %get-tuple-element.6) | data formatting | bytes 4194304

commit v7 on v6

--- a/solution.py
+++ b/solution.py
@@ -36,8 +36,8 @@
            a_ref, b_ref, in_s, av, bv, at, bn, psend, precv, prelay,
            ma_mine, ma_in, ma_sum, ma_all, mb_mine, mb_in, mb_sum, sta, stb,
            held, lo_sum, lo_mine, lo_in,
-           s1a_s, s1a_r, s1b_s, s1b_r, a_s, b_s, z_s, ma_s, mb_s, lo_s,
-           aga_r, rla_r, dd_r, ddf_r, agb_r, rlb_r, z1_r, z3_r, fr_r, mo_r, lo_r):
+           s1a_s, s1b_s, s1_r, a_s, b_s, z_s, ma_s, mb_s, lo_s,
+           ag_r, rl_r, dd_r, ddf_r, z1_r, z3_r, fr_r, mo_r, lo_r):
     zl, y, x, zh, c = (lax.axis_index(n) for n in ROW_COL)
 
     def scoped(f):
@@ -96,32 +96,31 @@
             cols = pl.ds(pl.multiple_of(ha * 4096 + yp * 1024 + k * AW, AW), AW)
             dst = av.at[n, x, y, c]
             if d:
-                send(a_ref.at[:, cols], dst, s1a_s, s1a_r.at[n], dev(y_=yp))
+                send(a_ref.at[:, cols], dst, s1a_s, s1_r.at[n], dev(y_=yp))
             else:
-                pltpu.make_async_copy(a_hbm.at[:, cols], dst, s1a_r.at[n]).start()
+                pltpu.make_async_copy(a_hbm.at[:, cols], dst, s1_r.at[n]).start()
         for r in (1, 2, 3, 7, 6, 5, 4, 0):
             px, pc = xc(r)
             cols = pl.ds(pl.multiple_of(px * 2048 + hb * 1024 + pc * 512 + k * BW, BW), BW)
             dst = bv.at[n, x, y, c]
             if r:
-                send(b_ref.at[:, cols], dst, s1b_s, s1b_r.at[n], dev(x_=px, c_=pc))
+                send(b_ref.at[:, cols], dst, s1b_s, s1_r.at[n], dev(x_=px, c_=pc))
             else:
-                pltpu.make_async_copy(b_hbm.at[:, cols], dst, s1b_r.at[n]).start()
+                pltpu.make_async_copy(b_hbm.at[:, cols], dst, s1_r.at[n]).start()
         return carry
 
     with jax.named_scope("stage1"):
         lax.fori_loop(0, N, stage1, 0)
 
     def s1_wait(n):
-        wait(av.at[n, x, :, c], s1a_r.at[n])
-        wait(bv.at[n, :, y], s1b_r.at[n])
+        wait(av.at[n, 0:2, :, c], s1_r.at[n])
 
     def own_part(n, up, down, k):
         for part, px, py in ((up, x1, y1), (down, x3, y3)):
             a = av.at[n, x, part, c]
-            send(a, a, a_s, aga_r.at[k], dev(x_=px))
+            send(a, a, a_s, ag_r.at[k], dev(x_=px))
             b = bv.at[n, part, y]
-            send(b, b, b_s, agb_r.at[k], dev(y_=py))
+            send(b, b, b_s, ag_r.at[k], dev(y_=py))
 
     ALL, LOW, HIGH = pl.ds(0, 4), pl.ds(0, 2), pl.ds(2, 2)
 
@@ -157,10 +156,10 @@
     def relay(n):
         for v, part, px in ((x3, LOW, x1), (x1, HIGH, x3)):
             a = av.at[n, v, part, c]
-            send(a, a, a_s, rla_r.at[n], dev(x_=px))
+            send(a, a, a_s, rl_r.at[n], dev(x_=px))
         for v, part, py in ((y3, LOW, y1), (y1, HIGH, y3)):
             b = bv.at[n, part, v]
-            send(b, b, b_s, rlb_r.at[n], dev(y_=py))
+            send(b, b, b_s, rl_r.at[n], dev(y_=py))
 
     def share(n, part3, part1):
         for v, part in ((x3, part3), (x1, part1)):
@@ -169,22 +168,19 @@
 
     @scoped
     def arrive(n):
-        wait(av.at[n, 0:2, :, c], aga_r.at[n])
-        wait(bv.at[n, :, 0:2], agb_r.at[n])
+        wait(av.at[n, :, :, c], ag_r.at[n])
         relay(n)
         share(n, ALL, ALL)
 
     @scoped
     def arrive_first(n):
-        wait(av.at[n, 0, :, c], aga_r.at[n])
-        wait(bv.at[n, :, 0], agb_r.at[n])
+        wait(av.at[n, 0:2, :, c], ag_r.at[n])
         relay(n)
         share(n, LOW, HIGH)
 
     @scoped
     def arrive_second(n):
-        wait(av.at[n, 0, :, c], aga_r.at[n + 1])
-        wait(bv.at[n, :, 0], agb_r.at[n + 1])
+        wait(av.at[n, 0:2, :, c], ag_r.at[n + 1])
         share(n, HIGH, LOW)
 
     def wait_and_sum(n, carry):
@@ -234,10 +230,9 @@
 
     @scoped
     def far(n):
-        wait(av.at[n, x2, :, c], rla_r.at[n])
+        wait(av.at[n, 0:2, :, c], rl_r.at[n])
         a = av.at[n, x2, :, c]
         send(a, a, a_s, ddf_r.at[n], dev(c_=other))
-        wait(bv.at[n, :, y2], rlb_r.at[n])
 
     def norm_a(n, lo, hi):
         def group(g, carry):
@@ -524,8 +519,8 @@
             vm((N, 2, AW), F32), vm((N, 2, BW), F32),
             vm((AW, 4 * BW), F32),
             vm((8, 128), F32), vm((1, 128), F32), vm((127, 1, 128), F32),
-            dma, dma((N,)), dma, dma((N,)), dma, dma, dma, dma, dma, dma,
-            dma((N + 1,)), dma((N,)), dma((N,)), dma((N,)), dma((N + 1,)), dma((N,)),
+            dma, dma, dma((N,)), dma, dma, dma, dma, dma, dma,
+            dma((N + 1,)), dma((N,)), dma((N,)), dma((N,)),
             dma((8,)), dma((5,)), dma((4, 2)), dma((5,)), dma,
         ],
         compiler_params=pltpu.CompilerParams(

time: 105 us -> 105 us (level)
  no operation moved by 1% of the time
where the time goes in v7:
time: 105 us
  Pallas kernels  102 us (97%)
  between operations  1.8 us (2%)
  local copies, waits for them, and re-layouts  1.32 us (1%)
    pallas_call x1, Pallas kernels, shards(): pl.pallas_call(lambda *refs: kernel(float(count), float(width), *refs), o...  102 us

profile of v7, /device:TPU:1, one launch (start us, length us, event | category | flops | bytes accessed | tf_op | source)
XLA Modules:
  0.0 104.8 jit_solution(17304079736716054213)
XLA Ops:
  0.6 101.6 %shard_map.41 = (f32[1024,512]{1,0:T(8,128)S(1)}, f32[1,1]{1,0:T(1,128)S(1)}) custom-call(bf16[96,8192]{1,0:T(8,128)(2,1)} %refs_0_.1, bf16[96,8192]{1,0:T(8,128)(2,1)} %refs_1_.1), custom_call_target="tpu_custom_call" | custom-call | tf_op jit(solution)/shard_map/pallas_call | solution.py:503
  102.3 1.3 %copy.6 = f32[1024,512]{1,0:T(8,128)} copy(f32[1024,512]{1,0:T(8,128)S(1)} %get-tuple-element.6) | data formatting | bytes 4194304
